TPU v7x, 128 devices: a whole 4x4x4 slice. The times are simulated.
128 devices in a mesh: rad: 8 (over z, core), ma: 16 (over y, x).
Axes of the slice: x: 4, y: 4, z: 4, core: 2. Of those that a mesh axis runs over, the one named last changes fastest.
Arguments:
- spectra: bfloat16 [128, 3, 2, 1024, 1024], P(('rad', 'ma')), may hold values from -0.19921875 to 0.19921875
- legendre: bfloat16 [1024, 1024, 512], P('ma', 'rad'), may hold values from -0.1875 to 0.1875
- selected: int32 [16], replicated, may hold values from 0 to 127, as said below
- m_order: int32 [1024], replicated, may hold values from 0 to 1023, each once
Outputs:
- shell_grid: float32 [16, 3, 2, 512, 3072], P(None, None, None, ('rad', 'ma'))
Inputs may be any that keep to these rules, and one draw needn't show every extreme that they name: `selected`: 16 distinct radii, in no particular order. `m_order`: every wavenumber 0 to 1023 stands in exactly one slot.
All inputs are finite; a program needn't handle non-finite values.
Results may differ from a plain program's by a relative error of at most 0.012.
Values may be sent and summed in bfloat16 or wider, within the bound.
A program may use at most 192 MiB of HBM per device.

v0:
```python
import jax
import jax.numpy as jnp
from jax import lax
from jax.sharding import Mesh
from jax.sharding import PartitionSpec as P

M = 1024
NPHI = 3072
FIELDS = 3
SEL = 16
RAD = ("rad_0", "rad_1")
RAD_MA = ("rad_0", "rad_1", "ma")


def reduced_to_own(pieces, axes, sequence):
    inside = pieces.shape[1:]
    pieces = pieces.reshape(*(lax.axis_size(a) for a in axes), *inside)
    pieces = jnp.moveaxis(pieces, sequence, range(len(axes))).reshape(-1, *inside)
    for k in sequence:
        pieces = lax.psum_scatter(pieces, axes[k], scatter_dimension=0, tiled=True)
    return pieces[0]


def in_blocks(array, dim, size):
    before, after = (array.shape[:dim], array.shape[dim + 1 :])
    return jnp.moveaxis(array.reshape(*before, size, -1, *after), dim, 0)


def scatter_axes(array, axes, sequence, dim):
    size = lax.axis_size(axes)
    return reduced_to_own(in_blocks(array, dim, size), axes, sequence)


def local(spectra, legendre, selected, m_order):
    rad_count = lax.axis_size(RAD)
    ma_count = lax.axis_size("ma")
    rad_index = lax.axis_index(RAD)
    ma_index = lax.axis_index("ma")
    slot_count = legendre.shape[0]
    part_len = legendre.shape[1]
    band_rows = legendre.shape[2] // rad_count
    owned = spectra.shape[0]
    channels = 2 * FIELDS
    width = SEL * channels
    local_spec = spectra.reshape(owned, channels, M, rad_count, part_len)
    local_spec = jnp.take(local_spec, m_order, axis=2)
    local_spec = local_spec.reshape(owned, channels, ma_count, slot_count, rad_count, part_len)
    local_spec = local_spec.transpose(4, 2, 0, 1, 3, 5)
    outgoing = local_spec.reshape(rad_count * ma_count, owned, channels, slot_count, part_len)
    received = lax.all_to_all(outgoing, RAD_MA, split_axis=0, concat_axis=0, tiled=True)
    received = received.reshape(-1, channels, slot_count, part_len)
    radii_total = received.shape[0]
    onehot = (selected[:, None] == jnp.arange(radii_total, dtype=jnp.int32)[None, :]).astype(
        jnp.bfloat16
    )
    coeffs = jnp.einsum("ij,jcsl->sicl", onehot, received, preferred_element_type=jnp.float32)
    coeffs = coeffs.reshape(slot_count, width, part_len)
    slot_m = lax.dynamic_slice_in_dim(m_order, ma_index * slot_count, slot_count)
    degree = rad_index * part_len + jnp.arange(part_len, dtype=jnp.int32)
    tri_mask = degree[None, :] >= slot_m[:, None]
    coeffs = jnp.where(tri_mask[:, None, :], coeffs, 0.0).astype(jnp.bfloat16)
    m_sign = (1 - 2 * (slot_m % 2)).astype(jnp.float32)
    parity_sign = m_sign[:, None] * (1 - 2 * (degree % 2)).astype(jnp.float32)[None, :]
    flipped = (coeffs.astype(jnp.float32) * parity_sign[:, None, :]).astype(jnp.bfloat16)
    north_sum = jnp.einsum("slt,sil->tsi", legendre, coeffs, preferred_element_type=jnp.float32)
    south_sum = jnp.einsum("slt,sil->tsi", legendre, flipped, preferred_element_type=jnp.float32)
    band = scatter_axes(
        jnp.stack([north_sum, south_sum], axis=1)
        .reshape(band_rows * lax.axis_size(RAD), 2, slot_count * width)
        .astype(jnp.bfloat16),
        RAD,
        (1, 0),
        0,
    ).astype(jnp.float32)
    latitude_sum = band.astype(jnp.bfloat16).reshape(band_rows, 2, slot_count, width)
    phase = m_order[:, None] * jnp.arange(NPHI, dtype=jnp.int32)[None, :] % NPHI
    angle = phase.astype(jnp.float32) * (2.0 * jnp.pi / NPHI)
    weight = jnp.where(m_order == 0, 1.0, 2.0).astype(jnp.float32)
    dft_table = jnp.concatenate(
        [weight[:, None] * jnp.cos(angle), -weight[:, None] * jnp.sin(angle)], axis=0
    ).astype(jnp.bfloat16)
    pieces = lax.all_to_all(latitude_sum, "ma", split_axis=0, concat_axis=2, tiled=True)
    row_block = pieces.shape[0]
    hemis = pieces.shape[1]
    arranged = pieces.reshape(row_block, hemis, M, SEL, FIELDS, 2).transpose(3, 4, 1, 0, 5, 2)
    arranged = arranged.reshape(-1, 2 * M)
    grid = jnp.dot(arranged, dft_table, preferred_element_type=jnp.float32)
    return grid.reshape(SEL, FIELDS, hemis, row_block, NPHI)


def solution(mesh):
    finer = Mesh(mesh.devices.reshape(4, 2, mesh.shape["ma"]), ("rad_0", "rad_1", "ma"))
    in_specs = (P(RAD_MA, None, None, None, None), P("ma", RAD, None), P(), P())
    out_specs = P(None, None, None, RAD_MA, None)
    return jax.shard_map(local, mesh=finer, in_specs=in_specs, out_specs=out_specs, check_vma=False)
```

profile of v0, /device:TPU:1, one launch (start us, length us, event | category | flops | bytes accessed | tf_op | source)
XLA Modules:
  0.0 541.6 jit_solution(12014291857333309675)
XLA Ops:
  7.9 11.9 %copy.55 = bf16[768,8,8,128]{3,2,1,0:T(8,128)(2,1)} copy(bf16[768,8,8,128]{3,1,2,0:T(8,128)(2,1)} %bitcast.63) | data formatting | bytes 25165824
  19.8 18.5 %gather_fusion = bf16[1024,6,8,128]{3,2,1,0:T(8,128)(2,1)} fusion(bf16[6,1024,8,128]{3,2,1,0:T(8,128)(2,1)} %bitcast.62, s32[1024]{0:T(1024)S(1)} %fusion.20), kind=kCustom, calls=%fused_computation | custom fusion | bytes 25169920 | tf_op jit(solution)/shard_map/jit(_take)/gather | solution.py:46
  38.2 10.4 %copy.39 = bf16[6,1024,8,128]{3,2,1,0:T(8,128)(2,1)} copy(bf16[6,1024,8,128]{3,2,0,1:T(8,128)(2,1)} %bitcast.61) | data formatting | bytes 25165824 | tf_op jit(solution)/shard_map/jit(_take)/gather | solution.py:46
  48.7 6.9 %select_bitcast_fusion = bf16[8,16,1,6,64,128]{5,0,4,1,3,2:T(8,128)(2,1)S(1)} fusion(bf16[1,6,16,64,8,128]{5,4,3,2,1,0:T(8,128)(2,1)} %bitcast.60, pred[16,64]{1,0:T(8,128)(4,1)S(1)} %broadcast_in_dim.47), kind=kLoop, calls=%fused_computation.17 | loop fusion | flops 6291456 | bytes 25166848 | tf_op jit(solution)/shard_map/transpose | solution.py:48
  55.6 7.0 %copy.40 = bf16[8,16,1,6,64,128]{5,4,3,1,0,2:T(8,128)(2,1)} copy(bf16[8,16,1,6,64,128]{5,0,4,1,3,2:T(8,128)(2,1)S(1)} %select_bitcast_fusion) | data formatting | bytes 25165824 | tf_op jit(solution)/shard_map/transpose | solution.py:48
  62.6 11.9 %all-to-all-start = ((bf16[128,1,6,64,128]{4,3,2,1,0:T(8,128)(2,1)}), bf16[128,1,6,64,128]{4,3,2,1,0:T(8,128)(2,1)}, u32[]{:S(2)}, u32[]{:S(2)}) async-start(bf16[128,1,6,64,128]{4,3,2,1,0:T(8,128)(2,1)} %bitcast.58), calls=%async_computation | async-start | bytes 25165824 | tf_op jit(solution)/shard_map/all_to_all | solution.py:50
  75.0 159.9 %all-to-all-done = bf16[128,1,6,64,128]{4,3,2,1,0:T(8,128)(2,1)} async-done(((bf16[128,1,6,64,128]{4,3,2,1,0:T(8,128)(2,1)}), bf16[128,1,6,64,128]{4,3,2,1,0:T(8,128)(2,1)}, u32[]{:S(2)}, u32[]{:S(2)}) %all-to-all-start) | async-done | bytes 12582944 | tf_op jit(solution)/shard_map/all_to_all | solution.py:50
  234.9 11.5 %fusion.12 = bf16[64,16,6,128]{3,1,0,2:T(8,128)(2,1)S(1)} fusion(bf16[128,1,6,64,128]{4,3,2,1,0:T(8,128)(2,1)} %all-to-all-done, s32[16]{0:T(128)S(1)} %copy-done.2), kind=kOutput, calls=%fused_computation.24 | convolution fusion | flops 201328640 | bytes 14155840 | tf_op jit(solution)/shard_map/ij,jcsl->sicl/dot_general | solution.py:56
  247.4 8.7 %convert_bitcast_fusion = bf16[512,64,96]{0,2,1:T(8,128)(2,1)} fusion(bf16[64,128,512]{2,1,0:T(8,128)(2,1)} %param.5, bf16[64,96,128]{2,0,1:T(8,128)(2,1)S(1)} %get-tuple-element.5), kind=kOutput, calls=%fused_computation.19 | convolution fusion | flops 808452096 | bytes 16252928 | tf_op jit(solution)/shard_map/slt,sil->tsi/dot_general | solution.py:66
  256.1 11.5 %copy.47 = bf16[512,64,96]{2,1,0:T(8,128)(2,1)} copy(bf16[512,64,96]{0,2,1:T(8,128)(2,1)} %convert_bitcast_fusion) | data formatting | bytes 12582912 | tf_op jit(solution)/shard_map/slt,sil->tsi/transpose | solution.py:66
  267.6 15.8 %stack.10 = bf16[4,2,64,1,6144]{4,2,1,0,3:T(8,128)(2,1)} reshape(bf16[512,64,96]{2,1,0:T(8,128)(2,1)} %copy.47) | data formatting | bytes 12582912 | tf_op jit(solution)/shard_map/stack | solution.py:68
  283.4 8.4 %convert_bitcast_fusion.1 = bf16[512,64,96]{0,2,1:T(8,128)(2,1)} fusion(bf16[64,128,512]{2,1,0:T(8,128)(2,1)} %param.5, bf16[64,96,128]{2,0,1:T(8,128)(2,1)S(1)} %get-tuple-element.6), kind=kOutput, calls=%fused_computation.20 | convolution fusion | flops 808452096 | bytes 16252928 | tf_op jit(solution)/shard_map/slt,sil->tsi/dot_general | solution.py:65
  291.8 11.5 %copy.45 = bf16[512,64,96]{2,1,0:T(8,128)(2,1)} copy(bf16[512,64,96]{0,2,1:T(8,128)(2,1)} %convert_bitcast_fusion.1) | data formatting | bytes 12582912 | tf_op jit(solution)/shard_map/slt,sil->tsi/transpose | solution.py:65
  303.4 15.8 %stack.9 = bf16[4,2,64,1,6144]{4,2,1,0,3:T(8,128)(2,1)} reshape(bf16[512,64,96]{2,1,0:T(8,128)(2,1)} %copy.45) | data formatting | bytes 12582912 | tf_op jit(solution)/shard_map/stack | solution.py:68
  319.1 6.1 %maximum_bitcast_fusion = bf16[2,4,64,2,6144]{4,2,0,1,3:T(8,128)(2,1)S(1)} fusion(bf16[4,2,64,1,6144]{4,2,1,0,3:T(8,128)(2,1)} %stack.10, bf16[4,2,64,1,6144]{4,2,1,0,3:T(8,128)(2,1)} %stack.9), kind=kLoop, calls=%fused_computation.4 | loop fusion | flops 6291456 | bytes 25165824 | tf_op jit(solution)/shard_map/transpose | solution.py:18
  325.3 5.5 %copy.48 = bf16[2,4,64,2,6144]{4,2,3,1,0:T(8,128)(2,1)} copy(bf16[2,4,64,2,6144]{4,2,0,1,3:T(8,128)(2,1)S(1)} %maximum_bitcast_fusion) | data formatting | bytes 25165824 | tf_op jit(solution)/shard_map/transpose | solution.py:18
  330.8 41.8 %reduce-scatter.3.cloned.1.call-done = bf16[4,64,2,6144]{3,1,2,0:T(8,128)(2,1)} async-done(((bf16[8,64,2,6144]{3,1,2,0:T(8,128)(2,1)}), bf16[4,64,2,6144]{3,1,2,0:T(8,128)(2,1)}) %reduce-scatter.3.cloned.1.call-update) | async-done | bytes 6291472 | tf_op jit(solution)/shard_map/reduce_scatter | solution.py:20
  372.7 68.9 %reduce-scatter.5.cloned.1.call-done = bf16[1,64,2,6144]{3,1,2,0:T(8,128)(2,1)} async-done(((bf16[4,64,2,6144]{3,1,2,0:T(8,128)(2,1)}), bf16[1,64,2,6144]{3,1,2,0:T(8,128)(2,1)}) %reduce-scatter.5.cloned.1.call-update) | async-done | bytes 1572880 | tf_op jit(solution)/shard_map/reduce_scatter | solution.py:20
  441.6 3.6 reshape.134
  446.7 6.5 %all-to-all-start.1 = ((bf16[64,2,64,96]{3,2,1,0:T(8,128)(2,1)}), bf16[64,2,64,96]{3,2,1,0:T(8,128)(2,1)S(1)}, u32[]{:S(2)}, u32[]{:S(2)}) async-start(bf16[64,2,64,96]{3,2,1,0:T(8,128)(2,1)} %copy.49), calls=%async_computation.3 | async-start | bytes 4194304 | tf_op jit(solution)/shard_map/all_to_all | solution.py:82
  453.3 55.7 %multiply_convert_fusion.1 = (bf16[1024,3072]{1,0:T(8,128)(2,1)}, bf16[1024,3072]{1,0:T(8,128)(2,1)}) fusion(s32[1024]{0:T(1024)S(1)} %copy-done.1, f32[1024]{0:T(1024)S(1)} %get-tuple-element.11, f32[1024]{0:T(1024)S(1)} %get-tuple-element.12), kind=kLoop, calls=%fused_computation.13 | loop fusion | flops 40894464 | bytes 12595200 | tf_op jit(solution)/shard_map/convert
  510.3 4.0 copy.50
  521.5 8.1 %fusion.2 = f32[16,3,2,4,3072]{4,0,3,2,1:T(8,128)S(1)} fusion(bf16[16,3,2,4,2048]{4,0,3,2,1:T(8,128)(2,1)S(1)} %dot_general.17, bf16[1024,3072]{1,0:T(8,128)(2,1)} %get-tuple-element.10, bf16[1024,3072]{1,0:T(8,128)(2,1)} %get-tuple-element.9), kind=kOutput, calls=%fused_computation.6 | convolution fusion | flops 4857004032 | bytes 18874368 | tf_op jit(solution)/shard_map/dot_general | solution.py:87
  529.6 5.2 copy.52
  (25 shorter events, 13.1 us)
Async XLA Ops:
  62.6 12.2 %copy-start.1 = (s32[1024]{0:T(1024)S(1)}, s32[1024]{0:T(1024)}, u32[]{:S(2)}) copy-start(s32[1024]{0:T(1024)} %param.7) | copy-start | bytes 12292
  62.6 172.3 %copy-start.2 = (s32[16]{0:T(128)S(1)}, s32[16]{0:T(128)}, u32[]{:S(2)}) copy-start(s32[16]{0:T(128)} %param.6) | copy-start | bytes 196
  62.6 172.3 %all-to-all-start = ((bf16[128,1,6,64,128]{4,3,2,1,0:T(8,128)(2,1)}), bf16[128,1,6,64,128]{4,3,2,1,0:T(8,128)(2,1)}, u32[]{:S(2)}, u32[]{:S(2)}) async-start(bf16[128,1,6,64,128]{4,3,2,1,0:T(8,128)(2,1)} %bitcast.58), calls=%async_computation | async-start | bytes 25165824 | tf_op jit(solution)/shard_map/all_to_all | solution.py:50
  74.5 298.1 %reduce-scatter.3.cloned.1.call-start = ((), (), s32[]{:S(2)}) async-start(), calls=%async_computation.4 | async-start | bytes 18874368 | tf_op jit(solution)/shard_map/reduce_scatter | solution.py:20
  330.8 110.8 %reduce-scatter.5.cloned.1.call-start = ((), (), s32[]{:S(2)}) async-start(), calls=%async_computation.5 | async-start | bytes 7864320 | tf_op jit(solution)/shard_map/reduce_scatter | solution.py:20
  446.7 62.3 %all-to-all-start.1 = ((bf16[64,2,64,96]{3,2,1,0:T(8,128)(2,1)}), bf16[64,2,64,96]{3,2,1,0:T(8,128)(2,1)S(1)}, u32[]{:S(2)}, u32[]{:S(2)}) async-start(bf16[64,2,64,96]{3,2,1,0:T(8,128)(2,1)} %copy.49), calls=%async_computation.3 | async-start | bytes 4194304 | tf_op jit(solution)/shard_map/all_to_all | solution.py:82
  509.0 1.3 copy-start
Sparse Core Ops, SparseCore 0:
  330.9 41.6 reduce-scatter.2
  375.1 66.4 reduce-scatter.4
where the time goes:
time: 543 us; the launch traced here: 542 us
  waiting for transfers between devices  271 us (50%)
  local copies, waits for them, and re-layouts  131 us (24%)
  other arithmetic  71 us (13%)
  matrix products  36.6 us (7%)
  starting transfers between devices  18.7 us (3%)
  between operations  13.5 us (2%)
    all_to_all x1, waiting for transfers between devices, local(): lax.all_to_all(outgoing, RAD_MA, split_axis=0, concat_axis=0, tiled=True)  160 us
    reduce_scatter x2, waiting for transfers between devices, reduced_to_own(): pieces = lax.psum_scatter(pieces, axes[k], scatter_dimension=0, tiled=True)  111 us
    another operation x1, other arithmetic  55.7 us
    another operation x2, local copies, waits for them, and re-layouts, local(): jnp.stack([north_sum, south_sum], axis=1)  31.6 us
    gather x2, local copies, waits for them, and re-layouts, local(): local_spec = jnp.take(local_spec, m_order, axis=2)  28.9 us
    unnamed x7, local copies, waits for them, and re-layouts  13.2 us
    all_to_all x1, starting transfers between devices, local(): lax.all_to_all(outgoing, RAD_MA, split_axis=0, concat_axis=0, tiled=True)  11.9 us
    transpose x1, local copies, waits for them, and re-layouts, local(): jnp.einsum('slt,sil->tsi', legendre, flipped, preferred_element_type=jnp....  11.5 us
  transfers between devices with their start and end apart: 4, of which 3 were waited for; matrix products, arithmetic and copies ran while one was open for 10% of the time, Pallas kernels for 0%

commit v1 on v0

v1 whole, which is shorter than its diff:
```python
import jax
import jax.numpy as jnp
from jax import lax
from jax.experimental import pallas as pl
from jax.experimental.pallas import tpu as pltpu
from jax.sharding import PartitionSpec as P

MESH = pl.DeviceIdType.MESH
M = 1024
NPHI = 3072
FIELDS = 3
SEL = 16
WIDTH = 2 * FIELDS * SEL
CHUNKS = 8
CS = 8


def synth_kernel(coef_ref, flip_ref, leg_ref, lat_ref, part, rcore, r1, r2,
                 core_s, core_r, z1_s, z1_r, z2_s, z2_r):
    rad = lax.axis_index("rad")
    core = lax.rem(rad, 2)
    z = rad // 2
    partner = z * 2 + 1 - core
    zu = lax.rem(z + 1, 4)
    zd = lax.rem(z + 3, 4)
    zo = lax.rem(z + 2, 4)
    up = zu * 2 + core
    down = zd * 2 + core

    barrier = pltpu.get_barrier_semaphore()
    for d in (partner, up, down):
        pl.semaphore_signal(barrier, inc=1, device_id={"rad": d}, device_id_type=MESH)
    pl.semaphore_wait(barrier, 3)

    def core_copy(k):
        return pltpu.make_async_remote_copy(
            src_ref=part.at[1 - core, k], dst_ref=rcore.at[k],
            send_sem=core_s.at[k], recv_sem=core_r.at[k],
            device_id={"rad": partner}, device_id_type=MESH)

    def z1_copy(k, side):
        return pltpu.make_async_remote_copy(
            src_ref=rcore.at[k, zo, side], dst_ref=r1.at[k, side],
            send_sem=z1_s.at[k, side], recv_sem=z1_r.at[k, side],
            device_id={"rad": up if side == 0 else down}, device_id_type=MESH)

    def z2_copy(k, side):
        return pltpu.make_async_remote_copy(
            src_ref=rcore.at[k, zu if side == 0 else zd], dst_ref=r2.at[k, side],
            send_sem=z2_s.at[k, side], recv_sem=z2_r.at[k, side],
            device_id={"rad": up if side == 0 else down}, device_id_type=MESH)

    low = lax.broadcasted_iota(jnp.int32, (WIDTH, 128), 1) < 64

    def legendre_chunk(k):
        def slot(j, carry):
            s = k * CS + j
            north = coef_ref[s]
            south = (north.astype(jnp.float32) * flip_ref[s]).astype(jnp.bfloat16)
            both = jnp.concatenate([north, south], axis=0)
            res = jnp.dot(both, leg_ref[s], preferred_element_type=jnp.float32)
            for q in range(4):
                nt = res[:WIDTH, 128 * q:128 * (q + 1)]
                st = res[WIDTH:, 128 * q:128 * (q + 1)]
                even = jnp.where(low, nt, pltpu.roll(st, 64, 1)).astype(jnp.bfloat16)
                odd = jnp.where(low, pltpu.roll(nt, 64, 1), st).astype(jnp.bfloat16)
                for side in range(2):
                    part[0, k, q, side, j] = even[48 * side:48 * (side + 1)]
                    part[1, k, q, side, j] = odd[48 * side:48 * (side + 1)]
            return carry
        lax.fori_loop(0, CS, slot, 0)

    def step(k, carry):
        @pl.when(k < CHUNKS)
        def _():
            legendre_chunk(k)
            core_copy(k).start()

        @pl.when((k >= 1) & (k < CHUNKS + 1))
        def _():
            c = k - 1
            core_copy(c).wait_recv()

            def add(n, carry):
                q = n // 2
                h = lax.rem(n, 2)
                a = part[core, c, q, h].astype(jnp.float32)
                b = rcore[c, q, h].astype(jnp.float32)
                rcore[c, q, h] = (a + b).astype(jnp.bfloat16)
                return carry
            lax.fori_loop(0, 8, add, 0)
            z1_copy(c, 0).start()
            z1_copy(c, 1).start()

        @pl.when((k >= 2) & (k < CHUNKS + 2))
        def _():
            c = k - 2
            for side in range(2):
                z1_copy(c, side).wait_recv()
                q = zu if side == 0 else zd
                a = rcore[c, q, side].astype(jnp.float32)
                b = r1[c, side].astype(jnp.float32)
                rcore[c, q, side] = (a + b).astype(jnp.bfloat16)
                z2_copy(c, side).start()

        @pl.when(k >= 3)
        def _():
            c = k - 3
            z2_copy(c, 0).wait_recv()
            z2_copy(c, 1).wait_recv()
            for side in range(2):
                total = rcore[c, z, side].astype(jnp.float32)
                total = total + r2[c, 0, side].astype(jnp.float32)
                total = total + r2[c, 1, side].astype(jnp.float32)
                lat_ref[c, side] = total.astype(jnp.bfloat16)
        return carry

    lax.fori_loop(0, CHUNKS + 3, step, 0)

    def drain(k, carry):
        core_copy(k).wait_send()
        for side in range(2):
            z1_copy(k, side).wait_send()
            z2_copy(k, side).wait_send()
        return carry
    lax.fori_loop(0, CHUNKS, drain, 0)


def synth(coef, flip, leg):
    bf = jnp.bfloat16
    vm = pl.BlockSpec(memory_space=pltpu.VMEM)
    return pl.pallas_call(
        synth_kernel,
        name="synth",
        out_shape=jax.ShapeDtypeStruct((CHUNKS, 2, CS, 48, 128), bf),
        in_specs=[vm, vm, vm],
        out_specs=vm,
        scratch_shapes=[
            pltpu.VMEM((2, CHUNKS, 4, 2, CS, 48, 128), bf),
            pltpu.VMEM((CHUNKS, 4, 2, CS, 48, 128), bf),
            pltpu.VMEM((CHUNKS, 2, CS, 48, 128), bf),
            pltpu.VMEM((CHUNKS, 2, 2, CS, 48, 128), bf),
            pltpu.SemaphoreType.DMA((CHUNKS,)),
            pltpu.SemaphoreType.DMA((CHUNKS,)),
            pltpu.SemaphoreType.DMA((CHUNKS, 2)),
            pltpu.SemaphoreType.DMA((CHUNKS, 2)),
            pltpu.SemaphoreType.DMA((CHUNKS, 2)),
            pltpu.SemaphoreType.DMA((CHUNKS, 2)),
        ],
        compiler_params=pltpu.CompilerParams(
            collective_id=1, has_side_effects=True, vmem_limit_bytes=56 * 1024 * 1024),
    )(coef, flip, leg)


PT = 256


def dft_kernel(lat_ref, c0_ref, s0_ref, rc_ref, rs_ref, out_ref, cs, sn, table):
    @pl.when(pl.program_id(0) == 0)
    def _():
        cs[...] = c0_ref[...]
        sn[...] = s0_ref[...]

    for half in range(PT // 128):
        def rows(b, carry, half=half):
            r = pl.ds(pl.multiple_of(b * 64, 64), 64)
            c = cs[r]
            s = sn[r]
            table[pl.ds(pl.multiple_of(b * 128, 128), 64), 128 * half:128 * (half + 1)] = c.astype(jnp.bfloat16)
            table[pl.ds(pl.multiple_of(b * 128 + 64, 64), 64), 128 * half:128 * (half + 1)] = (-s).astype(jnp.bfloat16)
            rc = rc_ref[r]
            rs = rs_ref[r]
            cs[r] = c * rc - s * rs
            sn[r] = s * rc + c * rs
            return carry
        lax.fori_loop(0, 16, rows, 0)
    lhs = jnp.concatenate([lat_ref[a] for a in range(16)], axis=1)
    acc = jnp.dot(lhs, table[...], preferred_element_type=jnp.float32)
    out_ref[...] = acc.reshape(out_ref.shape)


def dft(lat, c0, s0, rc, rs):
    full = lambda *dims: pl.BlockSpec(dims, lambda p: (0,) * len(dims))
    return pl.pallas_call(
        dft_kernel,
        name="dft",
        grid=(NPHI // PT,),
        out_shape=jax.ShapeDtypeStruct((SEL, FIELDS, 2, 4, NPHI), jnp.float32),
        in_specs=[full(16, 384, 128)] + [full(M, 128)] * 4,
        out_specs=pl.BlockSpec((SEL, FIELDS, 2, 4, PT), lambda p: (0, 0, 0, 0, p)),
        scratch_shapes=[
            pltpu.VMEM((M, 128), jnp.float32),
            pltpu.VMEM((M, 128), jnp.float32),
            pltpu.VMEM((2 * M, PT), jnp.bfloat16),
        ],
        compiler_params=pltpu.CompilerParams(
            dimension_semantics=("arbitrary",), vmem_limit_bytes=48 * 1024 * 1024),
    )(lat, c0, s0, rc, rs)


def local(spectra, legendre, selected, m_order):
    rad_count = lax.axis_size("rad")
    ma_count = lax.axis_size("ma")
    rad_index = lax.axis_index("rad")
    ma_index = lax.axis_index("ma")
    slot_count = legendre.shape[0]
    part_len = legendre.shape[1]
    channels = 2 * FIELDS

    step = 2.0 * jnp.pi / NPHI
    weight = jnp.where(m_order == 0, 1.0, 2.0).astype(jnp.float32)[:, None]
    phase = m_order[:, None] * jnp.arange(128, dtype=jnp.int32)[None, :] % NPHI
    angle = phase.astype(jnp.float32) * step
    turn = ((m_order * 128) % NPHI).astype(jnp.float32)[:, None] * step
    turn = jnp.broadcast_to(turn, (M, 128))
    c0, s0 = weight * jnp.cos(angle), weight * jnp.sin(angle)
    rc, rs = jnp.cos(turn), jnp.sin(turn)

    local_spec = spectra.reshape(channels, M, rad_count, part_len)
    local_spec = jnp.take(local_spec, m_order, axis=1)
    local_spec = local_spec.reshape(channels, ma_count, slot_count, rad_count, part_len)
    outgoing = local_spec.transpose(3, 1, 0, 2, 4)
    outgoing = outgoing.reshape(rad_count * ma_count, channels, slot_count, part_len)
    received = lax.all_to_all(outgoing, ("rad", "ma"), split_axis=0, concat_axis=0, tiled=True)
    onehot = (selected[:, None] == jnp.arange(rad_count * ma_count, dtype=jnp.int32)[None, :]).astype(jnp.bfloat16)
    coeffs = jnp.einsum("ij,jcsl->scil", onehot, received, preferred_element_type=jnp.float32)
    slot_m = lax.dynamic_slice_in_dim(m_order, ma_index * slot_count, slot_count)
    degree = rad_index * part_len + jnp.arange(part_len, dtype=jnp.int32)
    keep = degree[None, :] >= slot_m[:, None]
    coeffs = jnp.where(keep[:, None, None, :], coeffs, 0.0).astype(jnp.bfloat16)
    coeffs = coeffs.reshape(slot_count, WIDTH, part_len)
    flip = (1 - 2 * ((slot_m[:, None] + degree[None, :]) % 2)).astype(jnp.float32)[:, None, :]

    lat = synth(coeffs, flip, legendre)
    lat = lat.transpose(0, 2, 1, 3, 4).reshape(slot_count, FIELDS, 2, SEL, 2, ma_count, 4)
    lat = lat.transpose(5, 3, 1, 4, 6, 2, 0).reshape(ma_count, SEL * FIELDS * 2 * 4, 2 * slot_count)
    pieces = lax.all_to_all(lat, "ma", split_axis=0, concat_axis=0, tiled=True)
    return dft(pieces, c0, s0, rc, rs)


def solution(mesh):
    rad_ma = ("rad", "ma")
    in_specs = (P(rad_ma, None, None, None, None), P("ma", "rad", None), P(), P())
    out_specs = P(None, None, None, rad_ma, None)
    return jax.shard_map(local, mesh=mesh, in_specs=in_specs, out_specs=out_specs, check_vma=False)
```

time: 543 us -> 444 us (0.82)
  waiting for transfers between devices: 271 us -> 180 us
  Pallas kernels: 0 us -> 86.5 us
  other arithmetic: 71 us -> 11.4 us
  matrix products: 36.6 us -> 11.5 us
  between operations: 13.5 us -> 0.09 us
  starting transfers between devices: 18.7 us -> 31.4 us
  local copies, waits for them, and re-layouts: 131 us -> 120 us
    reduce_scatter x2 -> x0, waiting for transfers between devices: 111 us -> none  [reduced_to_own(): pieces = lax.psum_scatter(pieces, axes[k], scatter_dimension=0, tiled=True)]
    pallas_call x0 -> x2, Pallas kernels: none -> 86.5 us  [the longest x1 72.4 us: synth(): pl.pallas_call(synth_kernel, name='synth', out_shape=jax.ShapeDtypeStruct...]
    another operation x1 -> x0, other arithmetic: 55.7 us -> none
    another operation x2 -> x0, local copies, waits for them, and re-layouts: 31.6 us -> none  [local(): jnp.stack([north_sum, south_sum], axis=1)]
    dot_general x4 -> x1, matrix products: 36.6 us -> 11.5 us  [local(): jnp.einsum('ij,jcsl->scil', onehot, received, preferred_element_type=jnp....]
    reshape x3 -> x2, local copies, waits for them, and re-layouts: 8 us -> 29 us  [the longest x1 26.5 us: local(): lat.transpose(0, 2, 1, 3, 4)]
    all_to_all x2, waiting for transfers between devices: 160 us -> 180 us  [the longest x1 160 us: local(): lax.all_to_all(outgoing, ('rad', 'ma'), split_axis=0, concat_axis=0, tile...]
    all_to_all x2, starting transfers between devices: 18.4 us -> 31.4 us  [the longest x1 19.5 us: local(): pieces = lax.all_to_all(lat, 'ma', split_axis=0, concat_axis=0, tiled=True)]
  transfers between devices with their start and end apart: 4 -> 2, of which waited for: 3 -> 2; matrix products, arithmetic and copies ran while one was open for 10% -> 1% of each run, Pallas kernels for 0% -> 0%
where the time goes in v1:
time: 444 us; the launch traced here: 441 us
  waiting for transfers between devices  180 us (41%)
  local copies, waits for them, and re-layouts  120 us (27%)
  Pallas kernels  86.5 us (19%)
  starting transfers between devices  31.4 us (7%)
  matrix products  11.5 us (3%)
  other arithmetic  11.4 us (3%)
    all_to_all x1, waiting for transfers between devices, local(): lax.all_to_all(outgoing, ('rad', 'ma'), split_axis=0, concat_axis=0, tile...  160 us
    pallas_call x1, Pallas kernels, synth(): pl.pallas_call(synth_kernel, name='synth', out_shape=jax.ShapeDtypeStruct...  72.4 us
    transpose x1, local copies, waits for them, and re-layouts, local(): lat.transpose(5, 3, 1, 4, 6, 2, 0)  30.8 us
    gather x2, local copies, waits for them, and re-layouts, local(): local_spec = jnp.take(local_spec, m_order, axis=1)  28.9 us
    reshape x1, local copies, waits for them, and re-layouts, local(): lat.transpose(0, 2, 1, 3, 4)  26.5 us
    all_to_all x1, waiting for transfers between devices, local(): pieces = lax.all_to_all(lat, 'ma', split_axis=0, concat_axis=0, tiled=True)  20.9 us
    all_to_all x1, starting transfers between devices, local(): pieces = lax.all_to_all(lat, 'ma', split_axis=0, concat_axis=0, tiled=True)  19.5 us
    pallas_call x1, Pallas kernels, dft(): pl.pallas_call(dft_kernel, name='dft', grid=(NPHI // PT,), out_shape=jax....  14.1 us
  transfers between devices with their start and end apart: 2, of which 2 were waited for; matrix products, arithmetic and copies ran while one was open for 1% of the time, Pallas kernels for 0%

profile of v1, /device:TPU:1, one launch (start us, length us, event | category | flops | bytes accessed | tf_op | source)
XLA Modules:
  0.0 441.3 jit_solution(6371070341248518082)
XLA Ops:
  0.0 0.7 fusion.19
  0.7 0.7 compare_and_fusion
  1.4 11.9 %copy.27 = bf16[768,8,8,128]{3,2,1,0:T(8,128)(2,1)} copy(bf16[768,8,8,128]{3,1,2,0:T(8,128)(2,1)} %bitcast.27) | data formatting | bytes 25165824
  13.3 18.5 %gather_fusion = bf16[1024,6,8,128]{3,2,1,0:T(8,128)(2,1)} fusion(bf16[6,1024,8,128]{3,2,1,0:T(8,128)(2,1)} %bitcast.25, s32[1024]{0:T(1024)S(1)} %fusion.19), kind=kCustom, calls=%fused_computation | custom fusion | bytes 25169920 | tf_op jit(solution)/shard_map/jit(_take)/gather | solution.py:220
  31.7 10.4 %copy.20 = bf16[6,1024,8,128]{3,2,1,0:T(8,128)(2,1)} copy(bf16[6,1024,8,128]{3,2,0,1:T(8,128)(2,1)} %bitcast.24) | data formatting | bytes 25165824 | tf_op jit(solution)/shard_map/jit(_take)/gather | solution.py:220
  42.1 0.1 broadcast_in_dim.54
  42.2 6.9 %select_bitcast_fusion = bf16[8,16,6,64,128]{4,0,3,1,2:T(8,128)(2,1)S(1)} fusion(bf16[6,16,64,8,128]{4,3,2,1,0:T(8,128)(2,1)} %bitcast.23, pred[16,64]{1,0:T(8,128)(4,1)S(1)} %broadcast_in_dim.54), kind=kLoop, calls=%fused_computation.3 | loop fusion | flops 6291456 | bytes 25166848 | tf_op jit(solution)/shard_map/transpose | solution.py:222
  49.1 6.7 %copy.21 = bf16[8,16,6,64,128]{4,3,2,1,0:T(8,128)(2,1)} copy(bf16[8,16,6,64,128]{4,0,3,1,2:T(8,128)(2,1)S(1)} %select_bitcast_fusion) | data formatting | bytes 25165824 | tf_op jit(solution)/shard_map/transpose | solution.py:222
  55.8 11.9 %all-to-all-start = ((bf16[128,6,64,128]{3,2,1,0:T(8,128)(2,1)}), bf16[128,6,64,128]{3,2,1,0:T(8,128)(2,1)}, u32[]{:S(2)}, u32[]{:S(2)}) async-start(bf16[128,6,64,128]{3,2,1,0:T(8,128)(2,1)} %bitcast.22), calls=%async_computation | async-start | bytes 25165824 | tf_op jit(solution)/shard_map/all_to_all | solution.py:224
  67.9 0.8 fusion.13.flip_ref
  68.7 159.6 %all-to-all-done = bf16[128,6,64,128]{3,2,1,0:T(8,128)(2,1)} async-done(((bf16[128,6,64,128]{3,2,1,0:T(8,128)(2,1)}), bf16[128,6,64,128]{3,2,1,0:T(8,128)(2,1)}, u32[]{:S(2)}, u32[]{:S(2)}) %all-to-all-start) | async-done | bytes 12582944 | tf_op jit(solution)/shard_map/all_to_all | solution.py:224
  228.4 11.5 %fusion.2 = bf16[64,6,16,128]{3,2,0,1:T(8,128)(2,1)S(1)} fusion(pred[64,128]{1,0:T(8,128)(4,1)S(1)} %broadcast_compare_fusion, bf16[128,6,64,128]{3,2,1,0:T(8,128)(2,1)} %all-to-all-done, s32[16]{0:T(128)S(1)} %copy-done.1), kind=kOutput, calls=%fused_computation.5 | convolution fusion | flops 202901504 | bytes 14164032 | tf_op jit(solution)/shard_map/ij,jcsl->scil/dot_general | solution.py:226
  239.9 1.4 copy.23
  241.3 72.4 %synth.1 = bf16[8,2,8,48,128]{4,3,2,1,0:T(8,128)(2,1)} custom-call(bf16[64,96,128]{2,1,0:T(8,128)(2,1)} %bitcast.28, f32[64,1,128]{2,1,0:T(1,128)} %fusion.13.flip_ref, bf16[64,128,512]{2,1,0:T(8,128)(2,1)} %leg_ref.1), custom_call_target="tpu_custom_call" | custom-call | tf_op jit(solution)/shard_map/synth/pallas_call | solution.py:132
  313.7 10.6 %copy.24 = bf16[8,8,2,48,128]{3,2,4,1,0:T(2,128)(2,1)} copy(bf16[8,8,2,48,128]{4,3,1,2,0:T(8,128)(2,1)} %bitcast.29) | data formatting | bytes 3145728 | tf_op jit(solution)/shard_map/transpose | solution.py:235
  324.4 26.5 %reshape.138 = bf16[64,3,2,16,2,16,4]{3,2,1,6,5,4,0:T(2,128)(2,1)} reshape(bf16[8,8,2,48,128]{3,2,4,1,0:T(2,128)(2,1)} %copy.24) | data formatting | bytes 3145728 | tf_op jit(solution)/shard_map/reshape | solution.py:235
  350.8 30.8 %copy.25 = bf16[16,16,3,2,4,2,64]{6,5,4,3,2,1,0:T(2,128)(2,1)S(1)} copy(bf16[16,16,3,2,4,2,64]{1,5,2,4,0,3,6:T(2,128)(2,1)} %bitcast.26) | data formatting | bytes 3145728 | tf_op jit(solution)/shard_map/transpose | solution.py:236
  381.6 2.6 reshape.139
  384.2 19.5 %all-to-all-start.1 = ((bf16[16,384,128]{2,1,0:T(8,128)(2,1)}), bf16[16,384,128]{2,1,0:T(8,128)(2,1)S(1)}, u32[]{:S(2)}, u32[]{:S(2)}) async-start(bf16[16,384,128]{2,1,0:T(8,128)(2,1)} %reshape.139), calls=%async_computation.1 | async-start | bytes 3145728 | tf_op jit(solution)/shard_map/all_to_all | solution.py:237
  403.7 2.2 sine_multiply_fusion
  406.0 20.9 %all-to-all-done.1.lat_ref = bf16[16,384,128]{2,1,0:T(8,128)(2,1)S(1)} async-done(((bf16[16,384,128]{2,1,0:T(8,128)(2,1)}), bf16[16,384,128]{2,1,0:T(8,128)(2,1)S(1)}, u32[]{:S(2)}, u32[]{:S(2)}) %all-to-all-start.1) | async-done | bytes 1572896 | tf_op jit(solution)/shard_map/all_to_all | solution.py:237
  426.8 0.2 broadcast_in_dim.61.rc_ref
  427.0 0.2 broadcast_in_dim.62.rs_ref
  427.2 14.1 %dft.1 = f32[16,3,2,4,3072]{4,3,2,1,0:T(4,128)} custom-call(bf16[16,384,128]{2,1,0:T(8,128)(2,1)S(1)} %all-to-all-done.1.lat_ref, f32[1024,128]{1,0:T(8,128)S(1)} %get-tuple-element.6.c0_ref, f32[1024,128]{1,0:T(8,128)S(1)} %get-tuple-element.5.s0_ref, f32[1024,128]{1,0:T(8,128)S(1)} %broadcast_in_dim.61.rc_ref, f32[1024,128]{1,0:T(8,128)S(1)} %broadcast_in_dim.62.rs_ref), custom_call_target="tpu_custom_call" | custom-call | tf_op jit(solution)/shard_map/dft/pallas_call | solution.py:184
  (8 shorter events, 0.2 us)
Async XLA Ops:
  55.8 11.9 %copy-start = (s32[1024]{0:T(1024)S(1)}, s32[1024]{0:T(1024)}, u32[]{:S(2)}) copy-start(s32[1024]{0:T(1024)} %param.7) | copy-start | bytes 12292
  55.8 172.5 %copy-start.1 = (s32[16]{0:T(128)S(1)}, s32[16]{0:T(128)}, u32[]{:S(2)}) copy-start(s32[16]{0:T(128)} %param.6) | copy-start | bytes 196
  55.8 172.5 %all-to-all-start = ((bf16[128,6,64,128]{3,2,1,0:T(8,128)(2,1)}), bf16[128,6,64,128]{3,2,1,0:T(8,128)(2,1)}, u32[]{:S(2)}, u32[]{:S(2)}) async-start(bf16[128,6,64,128]{3,2,1,0:T(8,128)(2,1)} %bitcast.22), calls=%async_computation | async-start | bytes 25165824 | tf_op jit(solution)/shard_map/all_to_all | solution.py:224
  384.2 42.6 %all-to-all-start.1 = ((bf16[16,384,128]{2,1,0:T(8,128)(2,1)}), bf16[16,384,128]{2,1,0:T(8,128)(2,1)S(1)}, u32[]{:S(2)}, u32[]{:S(2)}) async-start(bf16[16,384,128]{2,1,0:T(8,128)(2,1)} %reshape.139), calls=%async_computation.1 | async-start | bytes 3145728 | tf_op jit(solution)/shard_map/all_to_all | solution.py:237

commit v2 on v1

--- a/solution.py
+++ b/solution.py
@@ -11,13 +11,15 @@
 FIELDS = 3
 SEL = 16
 WIDTH = 2 * FIELDS * SEL
-CHUNKS = 8
-CS = 8
-
-
-def synth_kernel(coef_ref, flip_ref, leg_ref, lat_ref, part, rcore, r1, r2,
-                 core_s, core_r, z1_s, z1_r, z2_s, z2_r):
+BLOCKS = 4
+CS = 16
+CHUNKS = FIELDS * BLOCKS
+
+
+def synth_kernel(coef_ref, flip_ref, leg_ref, lat_ref, part, rcore, r1, r2, latf, bsend,
+                 core_s, core_r, z1_s, z1_r, z2_s, z2_r, b_s, b_r):
     rad = lax.axis_index("rad")
+    ma = lax.axis_index("ma")
     core = lax.rem(rad, 2)
     z = rad // 2
     partner = z * 2 + 1 - core
@@ -30,7 +32,9 @@
     barrier = pltpu.get_barrier_semaphore()
     for d in (partner, up, down):
         pl.semaphore_signal(barrier, inc=1, device_id={"rad": d}, device_id_type=MESH)
-    pl.semaphore_wait(barrier, 3)
+    for n in range(1, 16):
+        pl.semaphore_signal(barrier, inc=1, device_id={"ma": lax.rem(ma + n, 16)}, device_id_type=MESH)
+    pl.semaphore_wait(barrier, 18)
 
     def core_copy(k):
         return pltpu.make_async_remote_copy(
@@ -50,25 +54,62 @@
             send_sem=z2_s.at[k, side], recv_sem=z2_r.at[k, side],
             device_id={"rad": up if side == 0 else down}, device_id_type=MESH)
 
-    low = lax.broadcasted_iota(jnp.int32, (WIDTH, 128), 1) < 64
+    def plane_copy(f, n):
+        to = lax.rem(ma + n, 16)
+        return pltpu.make_async_remote_copy(
+            src_ref=bsend.at[f, to], dst_ref=lat_ref.at[f, ma],
+            send_sem=b_s.at[f, n], recv_sem=b_r.at[f, n],
+            device_id={"ma": to}, device_id_type=MESH)
+
+    def plane_arrival(f, n):
+        src = lax.rem(ma + 16 - n, 16)
+        return pltpu.make_async_remote_copy(
+            src_ref=bsend.at[f, src], dst_ref=lat_ref.at[f, src],
+            send_sem=b_s.at[f, n], recv_sem=b_r.at[f, n],
+            device_id={"ma": src}, device_id_type=MESH)
+
+    low = lax.broadcasted_iota(jnp.int32, (32, 128), 1) < 64
+    top = lax.broadcasted_iota(jnp.int32, (8, 128), 0) < 4
 
     def legendre_chunk(k):
+        f = k // BLOCKS
+        first = lax.rem(k, BLOCKS) * CS
+
         def slot(j, carry):
-            s = k * CS + j
-            north = coef_ref[s]
+            s = first + j
+            north = coef_ref[f, s]
             south = (north.astype(jnp.float32) * flip_ref[s]).astype(jnp.bfloat16)
             both = jnp.concatenate([north, south], axis=0)
             res = jnp.dot(both, leg_ref[s], preferred_element_type=jnp.float32)
             for q in range(4):
-                nt = res[:WIDTH, 128 * q:128 * (q + 1)]
-                st = res[WIDTH:, 128 * q:128 * (q + 1)]
+                nt = res[:32, 128 * q:128 * (q + 1)]
+                st = res[32:, 128 * q:128 * (q + 1)]
                 even = jnp.where(low, nt, pltpu.roll(st, 64, 1)).astype(jnp.bfloat16)
                 odd = jnp.where(low, pltpu.roll(nt, 64, 1), st).astype(jnp.bfloat16)
                 for side in range(2):
-                    part[0, k, q, side, j] = even[48 * side:48 * (side + 1)]
-                    part[1, k, q, side, j] = odd[48 * side:48 * (side + 1)]
+                    part[0, k, q, side, j] = even[16 * side:16 * (side + 1)]
+                    part[1, k, q, side, j] = odd[16 * side:16 * (side + 1)]
             return carry
         lax.fori_loop(0, CS, slot, 0)
+
+    def turn(f):
+        def pair(n, carry):
+            halves = []
+            for i in (2 * n, 2 * n + 1):
+                block = jnp.concatenate(
+                    [latf[c, pl.ds(i, 64, stride=16), :] for c in range(2)], axis=0)
+                halves.append(block.T)
+            for b in range(8):
+                first, second = [], []
+                for x in halves:
+                    nt, st = x[8 * b:8 * b + 8], x[64 + 8 * b:64 + 8 * b + 8]
+                    first.append(jnp.where(top, nt, pltpu.roll(st, 4, 0)))
+                    second.append(jnp.where(top, pltpu.roll(nt, 4, 0), st))
+                bsend[f, 2 * b, n] = jnp.concatenate(first, axis=0).astype(jnp.bfloat16)
+                bsend[f, 2 * b + 1, n] = jnp.concatenate(second, axis=0).astype(jnp.bfloat16)
+            return carry
+        lax.fori_loop(0, 8, pair, 0)
+        lat_ref[f, ma] = bsend[f, ma]
 
     def step(k, carry):
         @pl.when(k < CHUNKS)
@@ -106,13 +147,25 @@
         @pl.when(k >= 3)
         def _():
             c = k - 3
+            f = c // BLOCKS
+            block = lax.rem(c, BLOCKS)
             z2_copy(c, 0).wait_recv()
             z2_copy(c, 1).wait_recv()
             for side in range(2):
                 total = rcore[c, z, side].astype(jnp.float32)
                 total = total + r2[c, 0, side].astype(jnp.float32)
                 total = total + r2[c, 1, side].astype(jnp.float32)
-                lat_ref[c, side] = total.astype(jnp.bfloat16)
+                rows = pl.ds(pl.multiple_of(block * 256, 256), 256)
+                latf[side, rows, :] = total.reshape(256, 128)
+
+            @pl.when(block == BLOCKS - 1)
+            def _():
+                turn(f)
+
+                def send(n, carry):
+                    plane_copy(f, n).start()
+                    return carry
+                lax.fori_loop(1, 16, send, 0)
         return carry
 
     lax.fori_loop(0, CHUNKS + 3, step, 0)
@@ -125,27 +178,35 @@
         return carry
     lax.fori_loop(0, CHUNKS, drain, 0)
 
+    def settle(n, carry):
+        for f in range(FIELDS):
+            plane_copy(f, n).wait_send()
+            plane_arrival(f, n).wait_recv()
+        return carry
+    lax.fori_loop(1, 16, settle, 0)
+
 
 def synth(coef, flip, leg):
     bf = jnp.bfloat16
     vm = pl.BlockSpec(memory_space=pltpu.VMEM)
+    dma = pltpu.SemaphoreType.DMA
     return pl.pallas_call(
         synth_kernel,
         name="synth",
-        out_shape=jax.ShapeDtypeStruct((CHUNKS, 2, CS, 48, 128), bf),
+        out_shape=jax.ShapeDtypeStruct((FIELDS, 16, 8, 16, 128), bf),
         in_specs=[vm, vm, vm],
         out_specs=vm,
         scratch_shapes=[
-            pltpu.VMEM((2, CHUNKS, 4, 2, CS, 48, 128), bf),
-            pltpu.VMEM((CHUNKS, 4, 2, CS, 48, 128), bf),
-            pltpu.VMEM((CHUNKS, 2, CS, 48, 128), bf),
-            pltpu.VMEM((CHUNKS, 2, 2, CS, 48, 128), bf),
-            pltpu.SemaphoreType.DMA((CHUNKS,)),
-            pltpu.SemaphoreType.DMA((CHUNKS,)),
-            pltpu.SemaphoreType.DMA((CHUNKS, 2)),
-            pltpu.SemaphoreType.DMA((CHUNKS, 2)),
-            pltpu.SemaphoreType.DMA((CHUNKS, 2)),
-            pltpu.SemaphoreType.DMA((CHUNKS, 2)),
+            pltpu.VMEM((2, CHUNKS, 4, 2, CS, 16, 128), bf),
+            pltpu.VMEM((CHUNKS, 4, 2, CS, 16, 128), bf),
+            pltpu.VMEM((CHUNKS, 2, CS, 16, 128), bf),
+            pltpu.VMEM((CHUNKS, 2, 2, CS, 16, 128), bf),
+            pltpu.VMEM((2, 1024, 128), jnp.float32),
+            pltpu.VMEM((FIELDS, 16, 8, 16, 128), bf),
+            dma((CHUNKS,)), dma((CHUNKS,)),
+            dma((CHUNKS, 2)), dma((CHUNKS, 2)),
+            dma((CHUNKS, 2)), dma((CHUNKS, 2)),
+            dma((FIELDS, 16)), dma((FIELDS, 16)),
         ],
         compiler_params=pltpu.CompilerParams(
             collective_id=1, has_side_effects=True, vmem_limit_bytes=56 * 1024 * 1024),
@@ -174,9 +235,10 @@
             sn[r] = s * rc + c * rs
             return carry
         lax.fori_loop(0, 16, rows, 0)
-    lhs = jnp.concatenate([lat_ref[a] for a in range(16)], axis=1)
-    acc = jnp.dot(lhs, table[...], preferred_element_type=jnp.float32)
-    out_ref[...] = acc.reshape(out_ref.shape)
+    for f in range(FIELDS):
+        lhs = jnp.concatenate([lat_ref[f, a].reshape(128, 128) for a in range(16)], axis=1)
+        acc = jnp.dot(lhs, table[...], preferred_element_type=jnp.float32)
+        out_ref[:, f] = acc.reshape(SEL, 2, 4, PT)
 
 
 def dft(lat, c0, s0, rc, rs):
@@ -186,7 +248,7 @@
         name="dft",
         grid=(NPHI // PT,),
         out_shape=jax.ShapeDtypeStruct((SEL, FIELDS, 2, 4, NPHI), jnp.float32),
-        in_specs=[full(16, 384, 128)] + [full(M, 128)] * 4,
+        in_specs=[full(FIELDS, 16, 8, 16, 128)] + [full(M, 128)] * 4,
         out_specs=pl.BlockSpec((SEL, FIELDS, 2, 4, PT), lambda p: (0, 0, 0, 0, p)),
         scratch_shapes=[
             pltpu.VMEM((M, 128), jnp.float32),
@@ -223,19 +285,16 @@
     outgoing = outgoing.reshape(rad_count * ma_count, channels, slot_count, part_len)
     received = lax.all_to_all(outgoing, ("rad", "ma"), split_axis=0, concat_axis=0, tiled=True)
     onehot = (selected[:, None] == jnp.arange(rad_count * ma_count, dtype=jnp.int32)[None, :]).astype(jnp.bfloat16)
-    coeffs = jnp.einsum("ij,jcsl->scil", onehot, received, preferred_element_type=jnp.float32)
+    coeffs = jnp.einsum("ij,jfcsl->fscil", onehot, received.reshape(-1, FIELDS, 2, slot_count, part_len), preferred_element_type=jnp.float32)
     slot_m = lax.dynamic_slice_in_dim(m_order, ma_index * slot_count, slot_count)
     degree = rad_index * part_len + jnp.arange(part_len, dtype=jnp.int32)
     keep = degree[None, :] >= slot_m[:, None]
-    coeffs = jnp.where(keep[:, None, None, :], coeffs, 0.0).astype(jnp.bfloat16)
-    coeffs = coeffs.reshape(slot_count, WIDTH, part_len)
+    coeffs = jnp.where(keep[None, :, None, None, :], coeffs, 0.0).astype(jnp.bfloat16)
+    coeffs = coeffs.reshape(FIELDS, slot_count, 2 * SEL, part_len)
     flip = (1 - 2 * ((slot_m[:, None] + degree[None, :]) % 2)).astype(jnp.float32)[:, None, :]
 
     lat = synth(coeffs, flip, legendre)
-    lat = lat.transpose(0, 2, 1, 3, 4).reshape(slot_count, FIELDS, 2, SEL, 2, ma_count, 4)
-    lat = lat.transpose(5, 3, 1, 4, 6, 2, 0).reshape(ma_count, SEL * FIELDS * 2 * 4, 2 * slot_count)
-    pieces = lax.all_to_all(lat, "ma", split_axis=0, concat_axis=0, tiled=True)
-    return dft(pieces, c0, s0, rc, rs)
+    return dft(lat, c0, s0, rc, rs)
 
 
 def solution(mesh):

time: 444 us -> 370 us (0.83)
  local copies, waits for them, and re-layouts: 120 us -> 62.6 us
  Pallas kernels: 86.5 us -> 125 us
  waiting for transfers between devices: 180 us -> 157 us
  starting transfers between devices: 31.4 us -> 11.9 us
  matrix products: 11.5 us -> 1.8 us
    transpose x2 -> x0, local copies, waits for them, and re-layouts: 41.4 us -> none  [the longest x1 30.8 us: local(): lat.transpose(5, 3, 1, 4, 6, 2, 0)]
    pallas_call x1, Pallas kernels: 72.4 us -> 110 us  [synth(): pl.pallas_call(synth_kernel, name='synth', out_shape=jax.ShapeDtypeStruct...]
    reshape x2 -> x0, local copies, waits for them, and re-layouts: 29 us -> none  [the longest x1 26.5 us: local(): lat.transpose(0, 2, 1, 3, 4)]
    all_to_all x1 -> x0, waiting for transfers between devices: 20.9 us -> none  [local(): pieces = lax.all_to_all(lat, 'ma', split_axis=0, concat_axis=0, tiled=True)]
    all_to_all x1 -> x0, starting transfers between devices: 19.5 us -> none  [local(): pieces = lax.all_to_all(lat, 'ma', split_axis=0, concat_axis=0, tiled=True)]
    all_to_all x0 -> x1, local copies, waits for them, and re-layouts: none -> 11.5 us  [local(): lax.all_to_all(outgoing, ('rad', 'ma'), split_axis=0, concat_axis=0, tile...]
    dot_general x1, matrix products: 11.5 us -> 1.8 us  [local(): jnp.einsum('ij,jfcsl->fscil', onehot, received.reshape(-1, FIELDS, 2, slo...]
    unnamed x5 -> x7, local copies, waits for them, and re-layouts: 11.9 us -> 13.3 us
  transfers between devices with their start and end apart: 2 -> 1, of which waited for: 2 -> 1; matrix products, arithmetic and copies ran while one was open for 1% -> 1% of each run, Pallas kernels for 0% -> 0%
where the time goes in v2:
time: 370 us
  waiting for transfers between devices  157 us (42%)
  Pallas kernels  125 us (34%)
  local copies, waits for them, and re-layouts  62.6 us (17%)
  starting transfers between devices  11.9 us (3%)
  other arithmetic  11.4 us (3%)
    all_to_all x1, waiting for transfers between devices, local(): lax.all_to_all(outgoing, ('rad', 'ma'), split_axis=0, concat_axis=0, tile...  157 us
    pallas_call x1, Pallas kernels, synth(): pl.pallas_call(synth_kernel, name='synth', out_shape=jax.ShapeDtypeStruct...  110 us
    gather x2, local copies, waits for them, and re-layouts, local(): local_spec = jnp.take(local_spec, m_order, axis=1)  28.9 us
    pallas_call x1, Pallas kernels, dft(): pl.pallas_call(dft_kernel, name='dft', grid=(NPHI // PT,), out_shape=jax....  14.3 us
    unnamed x7, local copies, waits for them, and re-layouts  13.3 us
    all_to_all x1, starting transfers between devices, local(): lax.all_to_all(outgoing, ('rad', 'ma'), split_axis=0, concat_axis=0, tile...  11.9 us
    all_to_all x1, local copies, waits for them, and re-layouts, local(): lax.all_to_all(outgoing, ('rad', 'ma'), split_axis=0, concat_axis=0, tile...  11.5 us
  transfers between devices with their start and end apart: 1, of which 1 were waited for; matrix products, arithmetic and copies ran while one was open for 1% of the time, Pallas kernels for 0%

profile of v2, /device:TPU:1, one launch (start us, length us, event | category | flops | bytes accessed | tf_op | source)
XLA Modules:
  0.0 369.7 jit_solution(14919143717603705817)
XLA Ops:
  0.0 0.7 fusion.15
  0.7 0.7 compare_and_fusion
  1.4 11.9 %copy.19 = bf16[768,8,8,128]{3,2,1,0:T(8,128)(2,1)} copy(bf16[768,8,8,128]{3,1,2,0:T(8,128)(2,1)} %bitcast.25) | data formatting | bytes 25165824
  13.3 18.5 %gather_fusion = bf16[1024,6,8,128]{3,2,1,0:T(8,128)(2,1)} fusion(bf16[6,1024,8,128]{3,2,1,0:T(8,128)(2,1)} %bitcast.24, s32[1024]{0:T(1024)S(1)} %fusion.15), kind=kCustom, calls=%fused_computation | custom fusion | bytes 25169920 | tf_op jit(solution)/shard_map/jit(_take)/gather | solution.py:282
  31.7 10.4 %copy.14 = bf16[6,1024,8,128]{3,2,1,0:T(8,128)(2,1)} copy(bf16[6,1024,8,128]{3,2,0,1:T(8,128)(2,1)} %bitcast.23) | data formatting | bytes 25165824 | tf_op jit(solution)/shard_map/jit(_take)/gather | solution.py:282
  42.1 0.1 broadcast_in_dim.54
  42.2 6.9 %select_bitcast_fusion = bf16[8,16,6,64,128]{4,0,3,1,2:T(8,128)(2,1)S(1)} fusion(bf16[6,16,64,8,128]{4,3,2,1,0:T(8,128)(2,1)} %bitcast.21, pred[16,64]{1,0:T(8,128)(4,1)S(1)} %broadcast_in_dim.54), kind=kLoop, calls=%fused_computation.1 | loop fusion | flops 6291456 | bytes 25166848 | tf_op jit(solution)/shard_map/transpose | solution.py:284
  49.1 7.0 %copy.15 = bf16[8,16,6,64,128]{4,3,2,1,0:T(8,128)(2,1)} copy(bf16[8,16,6,64,128]{4,0,3,1,2:T(8,128)(2,1)S(1)} %select_bitcast_fusion) | data formatting | bytes 25165824 | tf_op jit(solution)/shard_map/transpose | solution.py:284
  56.1 11.9 %all-to-all-start = ((bf16[128,6,64,128]{3,2,1,0:T(8,128)(2,1)}), bf16[128,6,64,128]{3,2,1,0:T(8,128)(2,1)}, u32[]{:S(2)}, u32[]{:S(2)}) async-start(bf16[128,6,64,128]{3,2,1,0:T(8,128)(2,1)} %bitcast.20), calls=%async_computation | async-start | bytes 25165824 | tf_op jit(solution)/shard_map/all_to_all | solution.py:286
  68.0 0.1 dynamic_slice.3
  68.1 0.1 broadcast_compare_fusion
  68.2 0.1 fusion.16
  68.3 0.8 fusion.9.flip_ref
  69.1 2.2 sine_multiply_fusion
  71.3 0.0 copy-start.2
  71.3 157.1 %all-to-all-done = bf16[128,6,64,128]{3,2,1,0:T(8,128)(2,1)} async-done(((bf16[128,6,64,128]{3,2,1,0:T(8,128)(2,1)}), bf16[128,6,64,128]{3,2,1,0:T(8,128)(2,1)}, u32[]{:S(2)}, u32[]{:S(2)}) %all-to-all-start) | async-done | bytes 12582944 | tf_op jit(solution)/shard_map/all_to_all | solution.py:286
  228.4 11.5 %copy.16 = bf16[128,6,64,128]{3,0,2,1:T(8,128)(2,1)S(1)} copy(bf16[128,6,64,128]{3,2,1,0:T(8,128)(2,1)} %all-to-all-done) | data formatting | bytes 25165824 | tf_op jit(solution)/shard_map/all_to_all | solution.py:286
  239.9 1.8 fusion
  241.7 1.4 copy.17
  243.1 110.5 %synth.1.lat_ref = bf16[3,16,8,16,128]{4,3,2,1,0:T(8,128)(2,1)} custom-call(bf16[3,64,32,128]{3,2,1,0:T(8,128)(2,1)} %bitcast.26, f32[64,1,128]{2,1,0:T(1,128)} %fusion.9.flip_ref, bf16[64,128,512]{2,1,0:T(8,128)(2,1)} %leg_ref.1), custom_call_target="tpu_custom_call" | custom-call | tf_op jit(solution)/shard_map/synth/pallas_call | solution.py:193
  353.6 0.2 broadcast_in_dim.61.rc_ref
  353.8 0.2 broadcast_in_dim.62.rs_ref
  354.0 1.4 copy-done
  355.4 14.3 %dft.1 = f32[16,3,2,4,3072]{4,3,2,1,0:T(4,128)} custom-call(bf16[3,16,8,16,128]{4,3,2,1,0:T(8,128)(2,1)S(1)} %copy-done, f32[1024,128]{1,0:T(8,128)S(1)} %get-tuple-element.6.c0_ref, f32[1024,128]{1,0:T(8,128)S(1)} %get-tuple-element.5.s0_ref, f32[1024,128]{1,0:T(8,128)S(1)} %broadcast_in_dim.61.rc_ref, f32[1024,128]{1,0:T(8,128)S(1)} %broadcast_in_dim.62.rs_ref), custom_call_target="tpu_custom_call" | custom-call | tf_op jit(solution)/shard_map/dft/pallas_call | solution.py:246
  (5 shorter events, 0.0 us)
Async XLA Ops:
  56.1 11.9 %copy-start.1 = (s32[1024]{0:T(1024)S(1)}, s32[1024]{0:T(1024)}, u32[]{:S(2)}) copy-start(s32[1024]{0:T(1024)} %param.7) | copy-start | bytes 12292
  56.1 172.3 %all-to-all-start = ((bf16[128,6,64,128]{3,2,1,0:T(8,128)(2,1)}), bf16[128,6,64,128]{3,2,1,0:T(8,128)(2,1)}, u32[]{:S(2)}, u32[]{:S(2)}) async-start(bf16[128,6,64,128]{3,2,1,0:T(8,128)(2,1)} %bitcast.20), calls=%async_computation | async-start | bytes 25165824 | tf_op jit(solution)/shard_map/all_to_all | solution.py:286
  71.3 168.6 %copy-start.2 = (s32[16]{0:T(128)S(1)}, s32[16]{0:T(128)}, u32[]{:S(2)}) copy-start(s32[16]{0:T(128)} %param.6) | copy-start | bytes 196
  354.0 1.4 copy-start

commit v3 on v2

--- a/solution.py
+++ b/solution.py
@@ -14,6 +14,201 @@
 BLOCKS = 4
 CS = 16
 CHUNKS = FIELDS * BLOCKS
+
+
+def relay_kernel(spec_ref, pick_ref, perm_ref, keep_ref, coef_ref, spec, asend, arecv, part, rcore, r1, r2,
+                 load, a_s, a_r, core_s, core_r, z1_s, z1_r, z2_s, z2_r):
+    rad = lax.axis_index("rad")
+    ma = lax.axis_index("ma")
+    core = lax.rem(rad, 2)
+    z = rad // 2
+    partner = z * 2 + 1 - core
+    zu = lax.rem(z + 1, 4)
+    zd = lax.rem(z + 3, 4)
+    zo = lax.rem(z + 2, 4)
+    up = zu * 2 + core
+    down = zd * 2 + core
+
+    def load_copy(ch):
+        return pltpu.make_async_copy(spec_ref.at[ch], spec.at[ch], load.at[ch])
+
+    for ch in range(2 * FIELDS):
+        load_copy(ch).start()
+
+    barrier = pltpu.get_barrier_semaphore()
+    for d in (partner, up, down):
+        pl.semaphore_signal(barrier, inc=1, device_id={"rad": d}, device_id_type=MESH)
+    for n in range(1, 16):
+        pl.semaphore_signal(barrier, inc=1, device_id={"ma": lax.rem(ma + n, 16)}, device_id_type=MESH)
+    pl.semaphore_wait(barrier, 18)
+
+    def a_copy(k, n):
+        to = lax.rem(ma + n, 16)
+        return pltpu.make_async_remote_copy(
+            src_ref=asend.at[lax.rem(k, 3), to], dst_ref=arecv.at[k, ma],
+            send_sem=a_s.at[k, n], recv_sem=a_r.at[k, n],
+            device_id={"ma": to}, device_id_type=MESH)
+
+    def a_arrival(k, n):
+        src = lax.rem(ma + 16 - n, 16)
+        return pltpu.make_async_remote_copy(
+            src_ref=asend.at[lax.rem(k, 3), src], dst_ref=arecv.at[k, src],
+            send_sem=a_s.at[k, n], recv_sem=a_r.at[k, n],
+            device_id={"ma": src}, device_id_type=MESH)
+
+    def core_copy(k):
+        return pltpu.make_async_remote_copy(
+            src_ref=part.at[1 - core, lax.rem(k, 3)], dst_ref=rcore.at[k],
+            send_sem=core_s.at[k], recv_sem=core_r.at[k],
+            device_id={"rad": partner}, device_id_type=MESH)
+
+    def z1_copy(k, side):
+        return pltpu.make_async_remote_copy(
+            src_ref=rcore.at[k, zo, side], dst_ref=r1.at[k, side],
+            send_sem=z1_s.at[k, side], recv_sem=z1_r.at[k, side],
+            device_id={"rad": up if side == 0 else down}, device_id_type=MESH)
+
+    def z2_copy(k, side):
+        return pltpu.make_async_remote_copy(
+            src_ref=rcore.at[k, zu if side == 0 else zd], dst_ref=r2.at[k, side],
+            send_sem=z2_s.at[k, side], recv_sem=z2_r.at[k, side],
+            device_id={"rad": up if side == 0 else down}, device_id_type=MESH)
+
+    def each(first, last, body):
+        def run(n, carry):
+            body(n)
+            return carry
+        lax.fori_loop(first, last, run, 0)
+
+    def gather(k):
+        f = k // BLOCKS
+        b = lax.rem(k, BLOCKS)
+        ring = lax.rem(k, 3)
+
+        @pl.when(b == 0)
+        def _():
+            load_copy(2 * f).wait()
+            load_copy(2 * f + 1).wait()
+
+        for c in range(2):
+            for n in range(4):
+                cols = slice(256 * n, 256 * (n + 1))
+                rows = jnp.dot(pick_ref[b], spec[2 * f + c, :, cols], preferred_element_type=jnp.float32)
+                asend[ring, :, c, :, cols] = rows.reshape(16, CS, 256).astype(jnp.bfloat16)
+
+    def compact(k):
+        ring = lax.rem(k, 3)
+        for c in range(2):
+            for n in range(4):
+                cols = slice(256 * n, 256 * (n + 1))
+                rows = arecv[k, :, c, :, cols].reshape(256, 256)
+                got = jnp.dot(perm_ref[...], rows, preferred_element_type=jnp.float32)
+                got = got.reshape(CS, 16, 256).astype(jnp.bfloat16)
+                part[0, ring, n, c] = got[:, :, :128]
+                part[1, ring, n, c] = got[:, :, 128:]
+
+    def step(k, carry):
+        @pl.when(k < CHUNKS)
+        def _():
+            @pl.when(k >= 3)
+            def _():
+                each(1, 16, lambda n: a_copy(k - 3, n).wait_send())
+            gather(k)
+            each(1, 16, lambda n: a_copy(k, n).start())
+            arecv[k, ma] = asend[lax.rem(k, 3), ma]
+
+        @pl.when((k >= 2) & (k < CHUNKS + 2))
+        def _():
+            c = k - 2
+            each(1, 16, lambda n: a_arrival(c, n).wait_recv())
+
+            @pl.when(c >= 3)
+            def _():
+                core_copy(c - 3).wait_send()
+            compact(c)
+            core_copy(c).start()
+
+        @pl.when((k >= 3) & (k < CHUNKS + 3))
+        def _():
+            c = k - 3
+            core_copy(c).wait_recv()
+
+            def add(n):
+                q = n // 2
+                h = lax.rem(n, 2)
+                a = part[core, lax.rem(c, 3), q, h].astype(jnp.float32)
+                b = rcore[c, q, h].astype(jnp.float32)
+                rcore[c, q, h] = (a + b).astype(jnp.bfloat16)
+            each(0, 8, add)
+            z1_copy(c, 0).start()
+            z1_copy(c, 1).start()
+
+        @pl.when((k >= 4) & (k < CHUNKS + 4))
+        def _():
+            c = k - 4
+            for side in range(2):
+                z1_copy(c, side).wait_recv()
+                q = zu if side == 0 else zd
+                a = rcore[c, q, side].astype(jnp.float32)
+                b = r1[c, side].astype(jnp.float32)
+                rcore[c, q, side] = (a + b).astype(jnp.bfloat16)
+                z2_copy(c, side).start()
+
+        @pl.when(k >= 5)
+        def _():
+            c = k - 5
+            z2_copy(c, 0).wait_recv()
+            z2_copy(c, 1).wait_recv()
+            for side in range(2):
+                total = rcore[c, z, side].astype(jnp.float32)
+                total = total + r2[c, 0, side].astype(jnp.float32)
+                total = total + r2[c, 1, side].astype(jnp.float32)
+                slots = pl.ds(lax.rem(c, BLOCKS) * CS, CS)
+                coef_ref[c, side] = (total * keep_ref[slots]).astype(jnp.bfloat16)
+        return carry
+
+    lax.fori_loop(0, CHUNKS + 5, step, 0)
+
+    def drain(k):
+        z1_copy(k, 0).wait_send()
+        z1_copy(k, 1).wait_send()
+        z2_copy(k, 0).wait_send()
+        z2_copy(k, 1).wait_send()
+    each(0, CHUNKS, drain)
+
+    def tail(k):
+        each(1, 16, lambda n: a_copy(k, n).wait_send())
+        core_copy(k).wait_send()
+    each(CHUNKS - 3, CHUNKS, tail)
+
+
+def relay(spec, pick, perm, keep):
+    bf = jnp.bfloat16
+    vm = pl.BlockSpec(memory_space=pltpu.VMEM)
+    dma = pltpu.SemaphoreType.DMA
+    return pl.pallas_call(
+        relay_kernel,
+        name="relay",
+        out_shape=jax.ShapeDtypeStruct((CHUNKS, 2, CS, SEL, 128), bf),
+        in_specs=[pl.BlockSpec(memory_space=pl.ANY), vm, vm, vm],
+        out_specs=vm,
+        scratch_shapes=[
+            pltpu.VMEM((2 * FIELDS, M, M), bf),
+            pltpu.VMEM((3, 16, 2, CS, M), bf),
+            pltpu.VMEM((CHUNKS, 16, 2, CS, M), bf),
+            pltpu.VMEM((2, 3, 4, 2, CS, SEL, 128), bf),
+            pltpu.VMEM((CHUNKS, 4, 2, CS, SEL, 128), bf),
+            pltpu.VMEM((CHUNKS, 2, CS, SEL, 128), bf),
+            pltpu.VMEM((CHUNKS, 2, 2, CS, SEL, 128), bf),
+            dma((2 * FIELDS,)),
+            dma((CHUNKS, 16)), dma((CHUNKS, 16)),
+            dma((CHUNKS,)), dma((CHUNKS,)),
+            dma((CHUNKS, 2)), dma((CHUNKS, 2)),
+            dma((CHUNKS, 2)), dma((CHUNKS, 2)),
+        ],
+        compiler_params=pltpu.CompilerParams(
+            collective_id=2, has_side_effects=True, vmem_limit_bytes=60 * 1024 * 1024),
+    )(spec, pick, perm, keep)
 
 
 def synth_kernel(coef_ref, flip_ref, leg_ref, lat_ref, part, rcore, r1, r2, latf, bsend,
@@ -77,7 +272,7 @@
 
         def slot(j, carry):
             s = first + j
-            north = coef_ref[f, s]
+            north = jnp.concatenate([coef_ref[k, 0, j], coef_ref[k, 1, j]], axis=0)
             south = (north.astype(jnp.float32) * flip_ref[s]).astype(jnp.bfloat16)
             both = jnp.concatenate([north, south], axis=0)
             res = jnp.dot(both, leg_ref[s], preferred_element_type=jnp.float32)
@@ -278,20 +473,18 @@
     c0, s0 = weight * jnp.cos(angle), weight * jnp.sin(angle)
     rc, rs = jnp.cos(turn), jnp.sin(turn)
 
-    local_spec = spectra.reshape(channels, M, rad_count, part_len)
-    local_spec = jnp.take(local_spec, m_order, axis=1)
-    local_spec = local_spec.reshape(channels, ma_count, slot_count, rad_count, part_len)
-    outgoing = local_spec.transpose(3, 1, 0, 2, 4)
-    outgoing = outgoing.reshape(rad_count * ma_count, channels, slot_count, part_len)
-    received = lax.all_to_all(outgoing, ("rad", "ma"), split_axis=0, concat_axis=0, tiled=True)
-    onehot = (selected[:, None] == jnp.arange(rad_count * ma_count, dtype=jnp.int32)[None, :]).astype(jnp.bfloat16)
-    coeffs = jnp.einsum("ij,jfcsl->fscil", onehot, received.reshape(-1, FIELDS, 2, slot_count, part_len), preferred_element_type=jnp.float32)
     slot_m = lax.dynamic_slice_in_dim(m_order, ma_index * slot_count, slot_count)
     degree = rad_index * part_len + jnp.arange(part_len, dtype=jnp.int32)
-    keep = degree[None, :] >= slot_m[:, None]
-    coeffs = jnp.where(keep[None, :, None, None, :], coeffs, 0.0).astype(jnp.bfloat16)
-    coeffs = coeffs.reshape(FIELDS, slot_count, 2 * SEL, part_len)
+    keep = (degree[None, :] >= slot_m[:, None]).astype(jnp.float32)[:, None, :]
     flip = (1 - 2 * ((slot_m[:, None] + degree[None, :]) % 2)).astype(jnp.float32)[:, None, :]
+
+    blocks = m_order.reshape(ma_count, BLOCKS, CS).transpose(1, 0, 2).reshape(BLOCKS, ma_count * CS)
+    pick = (blocks[:, :, None] == jnp.arange(M, dtype=jnp.int32)).astype(jnp.bfloat16)
+    lane = jnp.arange(16 * CS, dtype=jnp.int32)
+    row = lane[:, None]
+    owner = rad_index * ma_count + lane // CS
+    perm = (jnp.tile(selected, CS)[:, None] == owner[None, :]) & (row // SEL == lane[None, :] % CS)
+    coeffs = relay(spectra.reshape(channels, M, M), pick, perm.astype(jnp.bfloat16), keep)
 
     lat = synth(coeffs, flip, legendre)
     return dft(lat, c0, s0, rc, rs)

time: 370 us -> 288 us (0.78)
  waiting for transfers between devices: 157 us -> 0 us
  Pallas kernels: 125 us -> 275 us
  local copies, waits for them, and re-layouts: 62.6 us -> 4.14 us
  starting transfers between devices: 11.9 us -> 0 us
  other arithmetic: 11.4 us -> 7.7 us
    pallas_call x0 -> x1, Pallas kernels: none -> 169 us  [relay(): pl.pallas_call(relay_kernel, name='relay', out_shape=jax.ShapeDtypeStruct...]
    all_to_all x1 -> x0, waiting for transfers between devices: 157 us -> none  [local(): lax.all_to_all(outgoing, ('rad', 'ma'), split_axis=0, concat_axis=0, tile...]
    gather x2 -> x0, local copies, waits for them, and re-layouts: 28.9 us -> none  [local(): local_spec = jnp.take(local_spec, m_order, axis=1)]
    pallas_call x1, Pallas kernels: 110 us -> 92.2 us  [synth(): pl.pallas_call(synth_kernel, name='synth', out_shape=jax.ShapeDtypeStruct...]
    all_to_all x1 -> x0, starting transfers between devices: 11.9 us -> none  [local(): lax.all_to_all(outgoing, ('rad', 'ma'), split_axis=0, concat_axis=0, tile...]
    unnamed x7 -> x2, local copies, waits for them, and re-layouts: 13.3 us -> 1.4 us
    all_to_all x1 -> x0, local copies, waits for them, and re-layouts: 11.5 us -> none  [local(): lax.all_to_all(outgoing, ('rad', 'ma'), split_axis=0, concat_axis=0, tile...]
    transpose x1, local copies, waits for them, and re-layouts: 7 us -> 0.01 us  [local(): m_order.reshape(ma_count, BLOCKS, CS).transpose(1, 0, 2)]
  transfers between devices with their start and end apart: 1 -> 0, of which waited for: 1 -> 0; matrix products, arithmetic and copies ran while one was open for 1% -> 0% of each run, Pallas kernels for 0% -> 0%
where the time goes in v3:
time: 288 us; the launch traced here: 287 us
  Pallas kernels  275 us (95%)
  other arithmetic  7.7 us (3%)
  local copies, waits for them, and re-layouts  4.14 us (1%)
    pallas_call x1, Pallas kernels, relay(): pl.pallas_call(relay_kernel, name='relay', out_shape=jax.ShapeDtypeStruct...  169 us
    pallas_call x1, Pallas kernels, synth(): pl.pallas_call(synth_kernel, name='synth', out_shape=jax.ShapeDtypeStruct...  92.2 us
    pallas_call x1, Pallas kernels, dft(): pl.pallas_call(dft_kernel, name='dft', grid=(NPHI // PT,), out_shape=jax....  14.3 us

profile of v3, /device:TPU:1, one launch (start us, length us, event | category | flops | bytes accessed | tf_op | source)
XLA Modules:
  0.0 287.4 jit_solution(3051288459395777424)
XLA Ops:
  0.0 0.8 dynamic_slice.3
  0.8 0.7 tile.2
  1.4 0.1 eq.61
  1.5 0.7 fusion.12
  2.3 0.8 fusion.9.flip_ref
  3.1 0.7 compare_convert_fusion.keep_ref
  3.8 0.8 reshape.205
  4.6 0.1 eq.57
  4.7 0.8 and_convert_fusion.perm_ref
  5.4 0.2 broadcast_in_dim.15.rs_ref
  5.6 0.2 broadcast_in_dim.14.rc_ref
  5.8 2.9 %sine_multiply_fusion = (f32[1024,128]{1,0:T(8,128)S(1)}, f32[1024,128]{1,0:T(8,128)S(1)}) fusion(s32[1024]{0:T(1024)} %param.7, f32[1024]{0:T(1024)S(1)} %get-tuple-element.8), kind=kLoop, calls=%fused_computation.5 | loop fusion | flops 1441792 | bytes 1056768 | tf_op jit(solution)/shard_map/mul | solution.py:473
  8.8 1.7 fusion.pick_ref
  10.5 169.0 %relay.1.coef_ref = bf16[12,2,16,16,128]{4,3,2,1,0:T(8,128)(2,1)} custom-call(bf16[6,1024,1024]{2,1,0:T(8,128)(2,1)} %bitcast.2, bf16[4,256,1024]{2,1,0:T(8,128)(2,1)} %fusion.pick_ref, bf16[256,256]{1,0:T(8,128)(2,1)} %and_convert_fusion.perm_ref, f32[64,1,128]{2,1,0:T(1,128)} %compare_convert_fusion.keep_ref), custom_call_target="tpu_custom_call" | custom-call | tf_op jit(solution)/shard_map/relay/pallas_call | solution.py:189
  179.5 92.2 %synth.1.lat_ref = bf16[3,16,8,16,128]{4,3,2,1,0:T(8,128)(2,1)} custom-call(bf16[12,2,16,16,128]{4,3,2,1,0:T(8,128)(2,1)} %relay.1.coef_ref, f32[64,1,128]{2,1,0:T(1,128)} %fusion.9.flip_ref, bf16[64,128,512]{2,1,0:T(8,128)(2,1)} %leg_ref.1), custom_call_target="tpu_custom_call" | custom-call | tf_op jit(solution)/shard_map/synth/pallas_call | solution.py:388
  271.7 0.0 copy-start
  271.7 1.4 copy-done
  273.1 14.3 %dft.1 = f32[16,3,2,4,3072]{4,3,2,1,0:T(4,128)} custom-call(bf16[3,16,8,16,128]{4,3,2,1,0:T(8,128)(2,1)S(1)} %copy-done, f32[1024,128]{1,0:T(8,128)S(1)} %get-tuple-element.6.c0_ref, f32[1024,128]{1,0:T(8,128)S(1)} %get-tuple-element.5.s0_ref, f32[1024,128]{1,0:T(8,128)S(1)} %broadcast_in_dim.14.rc_ref, f32[1024,128]{1,0:T(8,128)S(1)} %broadcast_in_dim.15.rs_ref), custom_call_target="tpu_custom_call" | custom-call | tf_op jit(solution)/shard_map/dft/pallas_call | solution.py:441
  (4 shorter events, 0.0 us)
Async XLA Ops:
  271.7 1.4 copy-start

commit v4 on v2

v4 whole, which is shorter than its diff:
```python
import jax
import jax.numpy as jnp
from jax import lax
from jax.experimental import pallas as pl
from jax.experimental.pallas import tpu as pltpu
from jax.sharding import PartitionSpec as P

MESH = pl.DeviceIdType.MESH
M = 1024
NPHI = 3072
FIELDS = 3
SEL = 16
BLOCKS = 4
CS = 16
CHUNKS = FIELDS * BLOCKS


def flow_kernel(spec_ref, leg_ref, pick_ref, perm_ref, keep_ref, flip_ref, lat_ref,
                spec, leg, asend, arecv, coef,
                part1, core1, up1, in1, part2, core2, up2, in2, latf, bsend,
                load, leg_load, a_s, a_r, b_s, b_r, *rad_sems):
    rad = lax.axis_index("rad")
    ma = lax.axis_index("ma")
    core = lax.rem(rad, 2)
    z = rad // 2
    partner = z * 2 + 1 - core
    zu = lax.rem(z + 1, 4)
    zd = lax.rem(z + 3, 4)
    zo = lax.rem(z + 2, 4)
    up = zu * 2 + core
    down = zd * 2 + core

    def each(first, last, body):
        def run(n, carry):
            body(n)
            return carry
        lax.fori_loop(first, last, run, 0)

    def load_copy(f, c):
        return pltpu.make_async_copy(spec_ref.at[2 * f + c], spec.at[c], load.at[c])

    def leg_copy(k):
        rows = pl.ds(lax.rem(k, BLOCKS) * CS, CS)
        return pltpu.make_async_copy(leg_ref.at[rows], leg.at[lax.rem(k, 2)], leg_load.at[lax.rem(k, 2)])

    load_copy(0, 0).start()
    load_copy(0, 1).start()
    leg_copy(0).start()

    barrier = pltpu.get_barrier_semaphore()
    for d in (partner, up, down):
        pl.semaphore_signal(barrier, inc=1, device_id={"rad": d}, device_id_type=MESH)
    for n in range(1, 16):
        pl.semaphore_signal(barrier, inc=1, device_id={"ma": lax.rem(ma + n, 16)}, device_id_type=MESH)
    pl.semaphore_wait(barrier, 18)

    def a_copy(k, n):
        to = lax.rem(ma + n, 16)
        return pltpu.make_async_remote_copy(
            src_ref=asend.at[lax.rem(k, 3), to], dst_ref=arecv.at[k, ma],
            send_sem=a_s.at[k, n], recv_sem=a_r.at[k, n],
            device_id={"ma": to}, device_id_type=MESH)

    def a_arrival(k, n):
        src = lax.rem(ma + 16 - n, 16)
        return pltpu.make_async_remote_copy(
            src_ref=asend.at[lax.rem(k, 3), src], dst_ref=arecv.at[k, src],
            send_sem=a_s.at[k, n], recv_sem=a_r.at[k, n],
            device_id={"ma": src}, device_id_type=MESH)

    def plane_copy(f, n):
        to = lax.rem(ma + n, 16)
        return pltpu.make_async_remote_copy(
            src_ref=bsend.at[f, to], dst_ref=lat_ref.at[f, ma],
            send_sem=b_s.at[f, n], recv_sem=b_r.at[f, n],
            device_id={"ma": to}, device_id_type=MESH)

    def plane_arrival(f, n):
        src = lax.rem(ma + 16 - n, 16)
        return pltpu.make_async_remote_copy(
            src_ref=bsend.at[f, src], dst_ref=lat_ref.at[f, src],
            send_sem=b_s.at[f, n], recv_sem=b_r.at[f, n],
            device_id={"ma": src}, device_id_type=MESH)

    class Reduce:
        def __init__(self, part, rcore, r1, r2, sems):
            self.part, self.rcore, self.r1, self.r2 = part, rcore, r1, r2
            self.core_s, self.core_r, self.z1_s, self.z1_r, self.z2_s, self.z2_r = sems

        def core_copy(self, k):
            return pltpu.make_async_remote_copy(
                src_ref=self.part.at[1 - core, lax.rem(k, 3)], dst_ref=self.rcore.at[k],
                send_sem=self.core_s.at[k], recv_sem=self.core_r.at[k],
                device_id={"rad": partner}, device_id_type=MESH)

        def z1_copy(self, k, side):
            return pltpu.make_async_remote_copy(
                src_ref=self.rcore.at[k, zo, side], dst_ref=self.r1.at[k, side],
                send_sem=self.z1_s.at[k, side], recv_sem=self.z1_r.at[k, side],
                device_id={"rad": up if side == 0 else down}, device_id_type=MESH)

        def z2_copy(self, k, side):
            return pltpu.make_async_remote_copy(
                src_ref=self.rcore.at[k, zu if side == 0 else zd], dst_ref=self.r2.at[k, side],
                send_sem=self.z2_s.at[k, side], recv_sem=self.z2_r.at[k, side],
                device_id={"rad": up if side == 0 else down}, device_id_type=MESH)

        def free(self, k):
            @pl.when(k >= 3)
            def _():
                self.core_copy(k - 3).wait_send()

        def add(self, k):
            self.core_copy(k).wait_recv()

            def body(n):
                q = n // 2
                h = lax.rem(n, 2)
                a = self.part[core, lax.rem(k, 3), q, h].astype(jnp.float32)
                b = self.rcore[k, q, h].astype(jnp.float32)
                self.rcore[k, q, h] = (a + b).astype(jnp.bfloat16)
            each(0, 8, body)
            self.z1_copy(k, 0).start()
            self.z1_copy(k, 1).start()

        def forward(self, k):
            for side in range(2):
                self.z1_copy(k, side).wait_recv()
                q = zu if side == 0 else zd
                a = self.rcore[k, q, side].astype(jnp.float32)
                b = self.r1[k, side].astype(jnp.float32)
                self.rcore[k, q, side] = (a + b).astype(jnp.bfloat16)
                self.z2_copy(k, side).start()

        def finish(self, k, store):
            self.z2_copy(k, 0).wait_recv()
            self.z2_copy(k, 1).wait_recv()
            for side in range(2):
                total = self.rcore[k, z, side].astype(jnp.float32)
                total = total + self.r2[k, 0, side].astype(jnp.float32)
                total = total + self.r2[k, 1, side].astype(jnp.float32)
                store(side, total)

        def drain(self):
            def body(k):
                for side in range(2):
                    self.z1_copy(k, side).wait_send()
                    self.z2_copy(k, side).wait_send()
            each(0, CHUNKS, body)
            each(CHUNKS - 3, CHUNKS, lambda k: self.core_copy(k).wait_send())

    relay = Reduce(part1, core1, up1, in1, rad_sems[:6])
    sums = Reduce(part2, core2, up2, in2, rad_sems[6:])

    def gather(k):
        f = k // BLOCKS
        b = lax.rem(k, BLOCKS)
        ring = lax.rem(k, 3)

        @pl.when(b == 0)
        def _():
            load_copy(f, 0).wait()
            load_copy(f, 1).wait()

        for c in range(2):
            for n in range(4):
                cols = slice(256 * n, 256 * (n + 1))
                rows = jnp.dot(pick_ref[b], spec[c, :, cols], preferred_element_type=jnp.float32)
                asend[ring, :, c, :, cols] = rows.reshape(16, CS, 256).astype(jnp.bfloat16)

        @pl.when((b == BLOCKS - 1) & (f < FIELDS - 1))
        def _():
            load_copy(f + 1, 0).start()
            load_copy(f + 1, 1).start()

    def compact(k):
        ring = lax.rem(k, 3)
        for c in range(2):
            for n in range(4):
                cols = slice(256 * n, 256 * (n + 1))
                rows = arecv[k, :, c, :, cols].reshape(256, 256)
                got = jnp.dot(perm_ref[...], rows, preferred_element_type=jnp.float32)
                got = got.reshape(CS, 16, 256).astype(jnp.bfloat16)
                part1[0, ring, n, c] = got[:, :, :128]
                part1[1, ring, n, c] = got[:, :, 128:]

    low = lax.broadcasted_iota(jnp.int32, (32, 128), 1) < 64
    top = lax.broadcasted_iota(jnp.int32, (8, 128), 0) < 4

    def legendre(k):
        first = lax.rem(k, BLOCKS) * CS
        ring = lax.rem(k, 3)
        leg_copy(k).wait()

        @pl.when(k < CHUNKS - 1)
        def _():
            leg_copy(k + 1).start()

        def store(side, total):
            coef[side] = (total * keep_ref[pl.ds(first, CS)]).astype(jnp.bfloat16)
        relay.finish(k, store)

        def slot(j):
            north = jnp.concatenate([coef[0, j], coef[1, j]], axis=0)
            south = (north.astype(jnp.float32) * flip_ref[first + j]).astype(jnp.bfloat16)
            both = jnp.concatenate([north, south], axis=0)
            res = jnp.dot(both, leg[lax.rem(k, 2), j], preferred_element_type=jnp.float32)
            for q in range(4):
                nt = res[:32, 128 * q:128 * (q + 1)]
                st = res[32:, 128 * q:128 * (q + 1)]
                even = jnp.where(low, nt, pltpu.roll(st, 64, 1)).astype(jnp.bfloat16)
                odd = jnp.where(low, pltpu.roll(nt, 64, 1), st).astype(jnp.bfloat16)
                for side in range(2):
                    part2[0, ring, q, side, j] = even[16 * side:16 * (side + 1)]
                    part2[1, ring, q, side, j] = odd[16 * side:16 * (side + 1)]
        each(0, CS, slot)

    def turn(f):
        def pair(n):
            halves = []
            for i in (2 * n, 2 * n + 1):
                block = jnp.concatenate(
                    [latf[c, pl.ds(i, 64, stride=16), :] for c in range(2)], axis=0)
                halves.append(block.T)
            for b in range(8):
                first, second = [], []
                for x in halves:
                    nt, st = x[8 * b:8 * b + 8], x[64 + 8 * b:64 + 8 * b + 8]
                    first.append(jnp.where(top, nt, pltpu.roll(st, 4, 0)))
                    second.append(jnp.where(top, pltpu.roll(nt, 4, 0), st))
                bsend[f, 2 * b, n] = jnp.concatenate(first, axis=0).astype(jnp.bfloat16)
                bsend[f, 2 * b + 1, n] = jnp.concatenate(second, axis=0).astype(jnp.bfloat16)
        each(0, 8, pair)
        lat_ref[f, ma] = bsend[f, ma]

    def between(k, first, last, body):
        @pl.when((k >= first) & (k < last))
        def _():
            body()

    def step(k, carry):
        def send():
            @pl.when(k >= 3)
            def _():
                each(1, 16, lambda n: a_copy(k - 3, n).wait_send())
            gather(k)
            each(1, 16, lambda n: a_copy(k, n).start())
            arecv[k, ma] = asend[lax.rem(k, 3), ma]
        between(k, 0, CHUNKS, send)
        between(k, 3, CHUNKS + 3, lambda: relay.forward(k - 3))
        between(k, 4, CHUNKS + 4, lambda: sums.forward(k - 4))

        def arrive():
            c = k - 2
            each(1, 16, lambda n: a_arrival(c, n).wait_recv())
            relay.free(c)
            compact(c)
            relay.core_copy(c).start()
        between(k, 2, CHUNKS + 2, arrive)

        def transform():
            c = k - 3
            sums.free(c)
            legendre(c)
            sums.core_copy(c).start()
        between(k, 3, CHUNKS + 3, transform)
        between(k, 2, CHUNKS + 2, lambda: relay.add(k - 2))

        def settle():
            c = k - 4
            f = c // BLOCKS
            block = lax.rem(c, BLOCKS)
            rows = pl.ds(pl.multiple_of(block * 256, 256), 256)

            def store(side, total):
                latf[side, rows, :] = total.reshape(256, 128)
            sums.finish(c, store)

            @pl.when(block == BLOCKS - 1)
            def _():
                turn(f)
                each(1, 16, lambda n: plane_copy(f, n).start())
        between(k, 4, CHUNKS + 4, settle)
        between(k, 3, CHUNKS + 3, lambda: sums.add(k - 3))
        return carry

    lax.fori_loop(0, CHUNKS + 4, step, 0)

    relay.drain()
    sums.drain()
    for k in range(CHUNKS - 3, CHUNKS):
        each(1, 16, lambda n: a_copy(k, n).wait_send())

    def last(n):
        for f in range(FIELDS):
            plane_copy(f, n).wait_send()
            plane_arrival(f, n).wait_recv()
    each(1, 16, last)


def flow(spec, leg, pick, perm, keep, flip):
    bf = jnp.bfloat16
    vm = pl.BlockSpec(memory_space=pltpu.VMEM)
    hbm = pl.BlockSpec(memory_space=pl.ANY)
    dma = pltpu.SemaphoreType.DMA
    reduce_scratch = [
        pltpu.VMEM((2, 3, 4, 2, CS, SEL, 128), bf),
        pltpu.VMEM((CHUNKS, 4, 2, CS, SEL, 128), bf),
        pltpu.VMEM((CHUNKS, 2, CS, SEL, 128), bf),
        pltpu.VMEM((CHUNKS, 2, 2, CS, SEL, 128), bf),
    ]
    return pl.pallas_call(
        flow_kernel,
        name="flow",
        out_shape=jax.ShapeDtypeStruct((FIELDS, 16, 8, 16, 128), bf),
        in_specs=[hbm, hbm, vm, vm, vm, vm],
        out_specs=vm,
        scratch_shapes=[
            pltpu.VMEM((2, M, M), bf),
            pltpu.VMEM((2, CS, 128, 512), bf),
            pltpu.VMEM((3, 16, 2, CS, M), bf),
            pltpu.VMEM((CHUNKS, 16, 2, CS, M), bf),
            pltpu.VMEM((2, CS, SEL, 128), bf),
            *reduce_scratch, *reduce_scratch,
            pltpu.VMEM((2, 1024, 128), jnp.float32),
            pltpu.VMEM((FIELDS, 16, 8, 16, 128), bf),
            dma((2,)), dma((2,)),
            dma((CHUNKS, 16)), dma((CHUNKS, 16)),
            dma((FIELDS, 16)), dma((FIELDS, 16)),
            *([dma((CHUNKS,))] * 2 + [dma((CHUNKS, 2))] * 4) * 2,
        ],
        compiler_params=pltpu.CompilerParams(
            collective_id=1, has_side_effects=True, vmem_limit_bytes=67043328),
    )(spec, leg, pick, perm, keep, flip)


PT = 256


def dft_kernel(lat_ref, c0_ref, s0_ref, rc_ref, rs_ref, out_ref, cs, sn, table):
    @pl.when(pl.program_id(0) == 0)
    def _():
        cs[...] = c0_ref[...]
        sn[...] = s0_ref[...]

    for half in range(PT // 128):
        def rows(b, carry, half=half):
            r = pl.ds(pl.multiple_of(b * 64, 64), 64)
            c = cs[r]
            s = sn[r]
            table[pl.ds(pl.multiple_of(b * 128, 128), 64), 128 * half:128 * (half + 1)] = c.astype(jnp.bfloat16)
            table[pl.ds(pl.multiple_of(b * 128 + 64, 64), 64), 128 * half:128 * (half + 1)] = (-s).astype(jnp.bfloat16)
            rc = rc_ref[r]
            rs = rs_ref[r]
            cs[r] = c * rc - s * rs
            sn[r] = s * rc + c * rs
            return carry
        lax.fori_loop(0, 16, rows, 0)
    for f in range(FIELDS):
        lhs = jnp.concatenate([lat_ref[f, a].reshape(128, 128) for a in range(16)], axis=1)
        acc = jnp.dot(lhs, table[...], preferred_element_type=jnp.float32)
        out_ref[:, f] = acc.reshape(SEL, 2, 4, PT)


def dft(lat, c0, s0, rc, rs):
    full = lambda *dims: pl.BlockSpec(dims, lambda p: (0,) * len(dims))
    return pl.pallas_call(
        dft_kernel,
        name="dft",
        grid=(NPHI // PT,),
        out_shape=jax.ShapeDtypeStruct((SEL, FIELDS, 2, 4, NPHI), jnp.float32),
        in_specs=[full(FIELDS, 16, 8, 16, 128)] + [full(M, 128)] * 4,
        out_specs=pl.BlockSpec((SEL, FIELDS, 2, 4, PT), lambda p: (0, 0, 0, 0, p)),
        scratch_shapes=[
            pltpu.VMEM((M, 128), jnp.float32),
            pltpu.VMEM((M, 128), jnp.float32),
            pltpu.VMEM((2 * M, PT), jnp.bfloat16),
        ],
        compiler_params=pltpu.CompilerParams(
            dimension_semantics=("arbitrary",), vmem_limit_bytes=48 * 1024 * 1024),
    )(lat, c0, s0, rc, rs)


def local(spectra, legendre, selected, m_order):
    rad_count = lax.axis_size("rad")
    ma_count = lax.axis_size("ma")
    rad_index = lax.axis_index("rad")
    ma_index = lax.axis_index("ma")
    slot_count = legendre.shape[0]
    part_len = legendre.shape[1]
    channels = 2 * FIELDS

    step = 2.0 * jnp.pi / NPHI
    weight = jnp.where(m_order == 0, 1.0, 2.0).astype(jnp.float32)[:, None]
    phase = m_order[:, None] * jnp.arange(128, dtype=jnp.int32)[None, :] % NPHI
    angle = phase.astype(jnp.float32) * step
    turn = ((m_order * 128) % NPHI).astype(jnp.float32)[:, None] * step
    turn = jnp.broadcast_to(turn, (M, 128))
    c0, s0 = weight * jnp.cos(angle), weight * jnp.sin(angle)
    rc, rs = jnp.cos(turn), jnp.sin(turn)

    slot_m = lax.dynamic_slice_in_dim(m_order, ma_index * slot_count, slot_count)
    degree = rad_index * part_len + jnp.arange(part_len, dtype=jnp.int32)
    keep = (degree[None, :] >= slot_m[:, None]).astype(jnp.float32)[:, None, :]
    flip = (1 - 2 * ((slot_m[:, None] + degree[None, :]) % 2)).astype(jnp.float32)[:, None, :]

    blocks = m_order.reshape(ma_count, BLOCKS, CS).transpose(1, 0, 2).reshape(BLOCKS, ma_count * CS)
    pick = (blocks[:, :, None] == jnp.arange(M, dtype=jnp.int32)).astype(jnp.bfloat16)
    lane = jnp.arange(16 * CS, dtype=jnp.int32)
    row = lane[:, None]
    owner = rad_index * ma_count + lane // CS
    perm = (jnp.tile(selected, CS)[:, None] == owner[None, :]) & (row // SEL == lane[None, :] % CS)
    lat = flow(spectra.reshape(channels, M, M), legendre, pick, perm.astype(jnp.bfloat16), keep, flip)
    return dft(lat, c0, s0, rc, rs)


def solution(mesh):
    rad_ma = ("rad", "ma")
    in_specs = (P(rad_ma, None, None, None, None), P("ma", "rad", None), P(), P())
    out_specs = P(None, None, None, rad_ma, None)
    return jax.shard_map(local, mesh=mesh, in_specs=in_specs, out_specs=out_specs, check_vma=False)
```

time: 370 us -> 251 us (0.68)
  waiting for transfers between devices: 157 us -> 0 us
  Pallas kernels: 125 us -> 231 us
  local copies, waits for them, and re-layouts: 62.6 us -> 9.91 us
  starting transfers between devices: 11.9 us -> 0 us
    all_to_all x1 -> x0, waiting for transfers between devices: 157 us -> none  [local(): lax.all_to_all(outgoing, ('rad', 'ma'), split_axis=0, concat_axis=0, tile...]
    pallas_call x1, Pallas kernels: 110 us -> 217 us  [flow(): pl.pallas_call(flow_kernel, name='flow', out_shape=jax.ShapeDtypeStruct((...]
    gather x2 -> x0, local copies, waits for them, and re-layouts: 28.9 us -> none  [local(): local_spec = jnp.take(local_spec, m_order, axis=1)]
    all_to_all x1 -> x0, starting transfers between devices: 11.9 us -> none  [local(): lax.all_to_all(outgoing, ('rad', 'ma'), split_axis=0, concat_axis=0, tile...]
    all_to_all x1 -> x0, local copies, waits for them, and re-layouts: 11.5 us -> none  [local(): lax.all_to_all(outgoing, ('rad', 'ma'), split_axis=0, concat_axis=0, tile...]
    unnamed x7 -> x10, local copies, waits for them, and re-layouts: 13.3 us -> 5.57 us
    transpose x1, local copies, waits for them, and re-layouts: 7 us -> 0.01 us  [local(): m_order.reshape(ma_count, BLOCKS, CS).transpose(1, 0, 2)]
    transpose x1 -> x0, other arithmetic: 6.91 us -> none  [local(): outgoing = local_spec.transpose(3, 1, 0, 2, 4)]
  transfers between devices with their start and end apart: 1 -> 0, of which waited for: 1 -> 0; matrix products, arithmetic and copies ran while one was open for 1% -> 0% of each run, Pallas kernels for 0% -> 0%
where the time goes in v4:
time: 251 us; the launch traced here: 250 us
  Pallas kernels  231 us (92%)
  local copies, waits for them, and re-layouts  9.91 us (4%)
  other arithmetic  8.81 us (4%)
    pallas_call x1, Pallas kernels, flow(): pl.pallas_call(flow_kernel, name='flow', out_shape=jax.ShapeDtypeStruct((...  217 us
    pallas_call x1, Pallas kernels, dft(): pl.pallas_call(dft_kernel, name='dft', grid=(NPHI // PT,), out_shape=jax....  14.3 us
    unnamed x10, local copies, waits for them, and re-layouts  5.57 us

profile of v4, /device:TPU:1, one launch (start us, length us, event | category | flops | bytes accessed | tf_op | source)
XLA Modules:
  0.0 250.3 jit_solution(8279843375862968569)
XLA Ops:
  0.0 0.8 dynamic_slice.3
  0.8 0.7 tile.2
  1.4 0.1 eq.61
  1.5 0.7 fusion.12
  2.3 0.8 fusion.9.flip_ref
  3.1 0.7 compare_convert_fusion.keep_ref
  3.8 0.8 reshape.205
  4.6 0.1 eq.57
  4.7 0.8 and_convert_fusion.perm_ref
  5.4 1.0 broadcast_in_dim.15.rs_ref
  6.4 1.0 broadcast_in_dim.14.rc_ref
  7.4 4.0 %sine_multiply_fusion = (f32[1024,128]{1,0:T(8,128)}, f32[1024,128]{1,0:T(8,128)}) fusion(s32[1024]{0:T(1024)} %param.7, f32[1024]{0:T(1024)S(1)} %get-tuple-element.8), kind=kLoop, calls=%fused_computation.5 | loop fusion | flops 1441792 | bytes 1056768 | tf_op jit(solution)/shard_map/mul | solution.py:399
  11.4 1.7 fusion.pick_ref
  13.2 217.2 %flow.1.lat_ref = bf16[3,16,8,16,128]{4,3,2,1,0:T(8,128)(2,1)} custom-call(bf16[6,1024,1024]{2,1,0:T(8,128)(2,1)} %bitcast.2, bf16[64,128,512]{2,1,0:T(8,128)(2,1)} %leg_ref.1, bf16[4,256,1024]{2,1,0:T(8,128)(2,1)} %fusion.pick_ref, bf16[256,256]{1,0:T(8,128)(2,1)} %and_convert_fusion.perm_ref, f32[64,1,128]{2,1,0:T(1,128)} %compare_convert_fusion.keep_ref, ...), custom_call_target="tpu_custom_call" | custom-call | tf_op jit(solution)/shard_map/flow/pallas_call | solution.py:312
  230.4 0.0 copy-start
  230.4 1.4 copy-done
  231.8 0.0 copy-start.1
  231.8 1.0 copy-done.1
  232.9 0.0 copy-start.2
  232.9 1.0 copy-done.2
  233.9 0.0 copy-start.3
  233.9 1.0 copy-done.3
  234.9 1.0 copy-done.4
  236.0 14.3 %dft.1 = f32[16,3,2,4,3072]{4,3,2,1,0:T(4,128)} custom-call(bf16[3,16,8,16,128]{4,3,2,1,0:T(8,128)(2,1)S(1)} %copy-done, f32[1024,128]{1,0:T(8,128)S(1)} %copy-done.4, f32[1024,128]{1,0:T(8,128)S(1)} %copy-done.3, f32[1024,128]{1,0:T(8,128)S(1)} %copy-done.2, f32[1024,128]{1,0:T(8,128)S(1)} %copy-done.1), custom_call_target="tpu_custom_call" | custom-call | tf_op jit(solution)/shard_map/dft/pallas_call | solution.py:367
  (5 shorter events, 0.0 us)
Async XLA Ops:
  230.4 1.4 copy-start
  231.8 1.0 copy-start.1
  232.9 1.0 copy-start.2
  233.9 1.0 copy-start.3
  234.9 1.0 copy-start.4

commit v5 on v4

--- a/solution.py
+++ b/solution.py
@@ -15,10 +15,10 @@
 CHUNKS = FIELDS * BLOCKS
 
 
-def flow_kernel(spec_ref, leg_ref, pick_ref, perm_ref, keep_ref, flip_ref, lat_ref,
-                spec, leg, asend, arecv, coef,
+def flow_kernel(spec_ref, leg_ref, order_ref, chosen_ref, lat_ref, base_ref,
+                spec, leg, pick_ref, perm_ref, base, asend, arecv, coef,
                 part1, core1, up1, in1, part2, core2, up2, in2, latf, bsend,
-                load, leg_load, a_s, a_r, b_s, b_r, *rad_sems):
+                load, leg_load, base_sem, a_s, a_r, b_s, b_r, *rad_sems):
     rad = lax.axis_index("rad")
     ma = lax.axis_index("ma")
     core = lax.rem(rad, 2)
@@ -47,6 +47,39 @@
     load_copy(0, 1).start()
     leg_copy(0).start()
 
+    lane = lax.broadcasted_iota(jnp.int32, (16, 128), 1)
+    degree = rad * 128 + lax.broadcasted_iota(jnp.int32, (1, 128), 1)
+    for j in range(CS):
+        for half in range(2):
+            hit = (chosen_ref[...] == rad * 16 + 8 * half + lane // 16) & (lax.rem(lane, 16) == j)
+            perm_ref[16 * j:16 * (j + 1), 128 * half:128 * (half + 1)] = jnp.where(hit, 1.0, 0.0).astype(jnp.bfloat16)
+
+    def make_pick(b):
+        def body(a):
+            held = order_ref[pl.ds(a * 64 + b * CS, CS), :]
+            for n in range(8):
+                hit = jnp.where(held == lane + 128 * n, 1.0, 0.0).astype(jnp.bfloat16)
+                pick_ref[b, pl.ds(pl.multiple_of(a * 16, 16), 16), 128 * n:128 * (n + 1)] = hit
+        each(0, 16, body)
+
+    def base_copy():
+        return pltpu.make_async_copy(base, base_ref, base_sem)
+
+    def make_base():
+        def body(n):
+            rows = pl.ds(pl.multiple_of(n * 32, 32), 32)
+            held = order_ref[rows, :]
+            m = held.astype(jnp.float32)
+            point = lax.broadcasted_iota(jnp.int32, (32, 128), 1).astype(jnp.float32)
+            weight = jnp.where(held == 0, 1.0, 2.0)
+            for at, scale, where in ((m * point, weight, 0), (m * 128.0, 1.0, 2)):
+                at = at - NPHI * jnp.floor(at * (1.0 / NPHI))
+                angle = at * (2.0 * jnp.pi / NPHI)
+                base[where, rows, :] = scale * jnp.cos(angle)
+                base[where + 1, rows, :] = scale * jnp.sin(angle)
+        each(0, 32, body)
+        base_copy().start()
+
     barrier = pltpu.get_barrier_semaphore()
     for d in (partner, up, down):
         pl.semaphore_signal(barrier, inc=1, device_id={"rad": d}, device_id_type=MESH)
@@ -197,12 +230,14 @@
             leg_copy(k + 1).start()
 
         def store(side, total):
-            coef[side] = (total * keep_ref[pl.ds(first, CS)]).astype(jnp.bfloat16)
+            keep = degree >= order_ref[pl.ds(ma * 64 + first, CS), :]
+            coef[side] = jnp.where(keep[:, None, :], total, 0.0).astype(jnp.bfloat16)
         relay.finish(k, store)
 
         def slot(j):
             north = jnp.concatenate([coef[0, j], coef[1, j]], axis=0)
-            south = (north.astype(jnp.float32) * flip_ref[first + j]).astype(jnp.bfloat16)
+            odd = lax.rem(order_ref[pl.ds(ma * 64 + first + j, 1), :] + degree, 2)
+            south = jnp.where(odd == 1, -north.astype(jnp.float32), north.astype(jnp.float32)).astype(jnp.bfloat16)
             both = jnp.concatenate([north, south], axis=0)
             res = jnp.dot(both, leg[lax.rem(k, 2), j], preferred_element_type=jnp.float32)
             for q in range(4):
@@ -243,10 +278,17 @@
             @pl.when(k >= 3)
             def _():
                 each(1, 16, lambda n: a_copy(k - 3, n).wait_send())
+            @pl.when(k < BLOCKS)
+            def _():
+                make_pick(k)
             gather(k)
             each(1, 16, lambda n: a_copy(k, n).start())
             arecv[k, ma] = asend[lax.rem(k, 3), ma]
         between(k, 0, CHUNKS, send)
+
+        @pl.when(k == 6)
+        def _():
+            make_base()
         between(k, 3, CHUNKS + 3, lambda: relay.forward(k - 3))
         between(k, 4, CHUNKS + 4, lambda: sums.forward(k - 4))
 
@@ -286,6 +328,7 @@
 
     lax.fori_loop(0, CHUNKS + 4, step, 0)
 
+    base_copy().wait()
     relay.drain()
     sums.drain()
     for k in range(CHUNKS - 3, CHUNKS):
@@ -298,7 +341,7 @@
     each(1, 16, last)
 
 
-def flow(spec, leg, pick, perm, keep, flip):
+def flow(spec, leg, order, chosen):
     bf = jnp.bfloat16
     vm = pl.BlockSpec(memory_space=pltpu.VMEM)
     hbm = pl.BlockSpec(memory_space=pl.ANY)
@@ -312,106 +355,121 @@
     return pl.pallas_call(
         flow_kernel,
         name="flow",
-        out_shape=jax.ShapeDtypeStruct((FIELDS, 16, 8, 16, 128), bf),
-        in_specs=[hbm, hbm, vm, vm, vm, vm],
-        out_specs=vm,
+        out_shape=[jax.ShapeDtypeStruct((FIELDS, 16, 8, 16, 128), bf),
+                   jax.ShapeDtypeStruct((4, M, 128), jnp.float32)],
+        in_specs=[hbm, hbm, vm, vm],
+        out_specs=[vm, hbm],
         scratch_shapes=[
             pltpu.VMEM((2, M, M), bf),
             pltpu.VMEM((2, CS, 128, 512), bf),
+            pltpu.VMEM((BLOCKS, 16 * CS, M), bf),
+            pltpu.VMEM((16 * CS, 16 * CS), bf),
+            pltpu.VMEM((4, M, 128), jnp.float32),
             pltpu.VMEM((3, 16, 2, CS, M), bf),
             pltpu.VMEM((CHUNKS, 16, 2, CS, M), bf),
             pltpu.VMEM((2, CS, SEL, 128), bf),
             *reduce_scratch, *reduce_scratch,
             pltpu.VMEM((2, 1024, 128), jnp.float32),
             pltpu.VMEM((FIELDS, 16, 8, 16, 128), bf),
-            dma((2,)), dma((2,)),
+            dma((2,)), dma((2,)), dma(()),
             dma((CHUNKS, 16)), dma((CHUNKS, 16)),
             dma((FIELDS, 16)), dma((FIELDS, 16)),
             *([dma((CHUNKS,))] * 2 + [dma((CHUNKS, 2))] * 4) * 2,
         ],
         compiler_params=pltpu.CompilerParams(
             collective_id=1, has_side_effects=True, vmem_limit_bytes=67043328),
-    )(spec, leg, pick, perm, keep, flip)
+    )(spec, leg, order, chosen)
 
 
 PT = 256
-
-
-def dft_kernel(lat_ref, c0_ref, s0_ref, rc_ref, rs_ref, out_ref, cs, sn, table):
-    @pl.when(pl.program_id(0) == 0)
-    def _():
-        cs[...] = c0_ref[...]
-        sn[...] = s0_ref[...]
-
-    for half in range(PT // 128):
-        def rows(b, carry, half=half):
-            r = pl.ds(pl.multiple_of(b * 64, 64), 64)
-            c = cs[r]
-            s = sn[r]
-            table[pl.ds(pl.multiple_of(b * 128, 128), 64), 128 * half:128 * (half + 1)] = c.astype(jnp.bfloat16)
-            table[pl.ds(pl.multiple_of(b * 128 + 64, 64), 64), 128 * half:128 * (half + 1)] = (-s).astype(jnp.bfloat16)
-            rc = rc_ref[r]
-            rs = rs_ref[r]
-            cs[r] = c * rc - s * rs
-            sn[r] = s * rc + c * rs
-            return carry
-        lax.fori_loop(0, 16, rows, 0)
+STEPS = NPHI // 2 // PT
+
+
+def dft_kernel(lat_ref, base_ref, out_ref, lhs, cs, sn, ctab, stab, held):
+    low = lax.broadcasted_iota(jnp.int32, (128, 128), 1) < 64
     for f in range(FIELDS):
-        lhs = jnp.concatenate([lat_ref[f, a].reshape(128, 128) for a in range(16)], axis=1)
-        acc = jnp.dot(lhs, table[...], preferred_element_type=jnp.float32)
-        out_ref[:, f] = acc.reshape(SEL, 2, 4, PT)
-
-
-def dft(lat, c0, s0, rc, rs):
-    full = lambda *dims: pl.BlockSpec(dims, lambda p: (0,) * len(dims))
+        rows = slice(128 * f, 128 * (f + 1))
+        for b in range(8):
+            x0 = lat_ref[f, 2 * b].reshape(128, 128).astype(jnp.float32)
+            x1 = lat_ref[f, 2 * b + 1].reshape(128, 128).astype(jnp.float32)
+            cols = slice(128 * b, 128 * (b + 1))
+            lhs[0, rows, cols] = jnp.where(low, x0, pltpu.roll(x1, 64, 1)).astype(jnp.bfloat16)
+            lhs[1, rows, cols] = jnp.where(low, pltpu.roll(x0, 64, 1), x1).astype(jnp.bfloat16)
+    cs[...] = base_ref[0]
+    sn[...] = base_ref[1]
+    lane = lax.broadcasted_iota(jnp.int32, (128, 128), 1)
+    back = lax.rem(128 - lane, 128)
+
+    def put(f, tile, x):
+        cols = pl.ds(pl.multiple_of(tile * 128, 128), 128)
+        out_ref[:, f, :, :, cols] = x.reshape(SEL, 2, 4, 128)
+
+    def step(u, carry):
+        for half in range(2):
+            cols = slice(128 * half, 128 * (half + 1))
+
+            def rows(b, carry, cols=cols):
+                r = pl.ds(pl.multiple_of(b * 64, 64), 64)
+                c = cs[r]
+                s = sn[r]
+                ctab[r, cols] = c.astype(jnp.bfloat16)
+                stab[r, cols] = (-s).astype(jnp.bfloat16)
+                rc = base_ref[2, r]
+                rs = base_ref[3, r]
+                cs[r] = c * rc - s * rs
+                sn[r] = s * rc + c * rs
+                return carry
+            lax.fori_loop(0, 16, rows, 0)
+        for f in range(FIELDS):
+            at = slice(128 * f, 128 * (f + 1))
+            even = jnp.dot(lhs[0, at], ctab[...], preferred_element_type=jnp.float32)
+            odd = jnp.dot(lhs[1, at], stab[...], preferred_element_type=jnp.float32)
+            plus = even + odd
+            less = even - odd
+            first, second = less[:, :128], less[:, 128:]
+
+            @pl.when(u > 0)
+            def _():
+                put(f, 24 - 2 * u, jnp.where(lane == 0, first, held[f]))
+
+            @pl.when(u < STEPS)
+            def _():
+                put(f, 2 * u, plus[:, :128])
+                put(f, 2 * u + 1, plus[:, 128:])
+                turned = jnp.take_along_axis(first, back, axis=1)
+                put(f, 23 - 2 * u, jnp.where(lane == 0, second, turned))
+                held[f] = jnp.take_along_axis(second, back, axis=1)
+        return carry
+
+    lax.fori_loop(0, STEPS + 1, step, 0)
+
+
+def dft(lat, base):
+    vm = pl.BlockSpec(memory_space=pltpu.VMEM)
+    f32 = jnp.float32
     return pl.pallas_call(
         dft_kernel,
         name="dft",
-        grid=(NPHI // PT,),
-        out_shape=jax.ShapeDtypeStruct((SEL, FIELDS, 2, 4, NPHI), jnp.float32),
-        in_specs=[full(FIELDS, 16, 8, 16, 128)] + [full(M, 128)] * 4,
-        out_specs=pl.BlockSpec((SEL, FIELDS, 2, 4, PT), lambda p: (0, 0, 0, 0, p)),
+        out_shape=jax.ShapeDtypeStruct((SEL, FIELDS, 2, 4, NPHI), f32),
+        in_specs=[vm, vm],
+        out_specs=vm,
         scratch_shapes=[
-            pltpu.VMEM((M, 128), jnp.float32),
-            pltpu.VMEM((M, 128), jnp.float32),
-            pltpu.VMEM((2 * M, PT), jnp.bfloat16),
+            pltpu.VMEM((2, FIELDS * 128, M), jnp.bfloat16),
+            pltpu.VMEM((M, 128), f32),
+            pltpu.VMEM((M, 128), f32),
+            pltpu.VMEM((M, PT), jnp.bfloat16),
+            pltpu.VMEM((M, PT), jnp.bfloat16),
+            pltpu.VMEM((FIELDS, 128, 128), f32),
         ],
-        compiler_params=pltpu.CompilerParams(
-            dimension_semantics=("arbitrary",), vmem_limit_bytes=48 * 1024 * 1024),
-    )(lat, c0, s0, rc, rs)
+        compiler_params=pltpu.CompilerParams(vmem_limit_bytes=48 * 1024 * 1024),
+    )(lat, base)
 
 
 def local(spectra, legendre, selected, m_order):
-    rad_count = lax.axis_size("rad")
-    ma_count = lax.axis_size("ma")
-    rad_index = lax.axis_index("rad")
-    ma_index = lax.axis_index("ma")
-    slot_count = legendre.shape[0]
-    part_len = legendre.shape[1]
-    channels = 2 * FIELDS
-
-    step = 2.0 * jnp.pi / NPHI
-    weight = jnp.where(m_order == 0, 1.0, 2.0).astype(jnp.float32)[:, None]
-    phase = m_order[:, None] * jnp.arange(128, dtype=jnp.int32)[None, :] % NPHI
-    angle = phase.astype(jnp.float32) * step
-    turn = ((m_order * 128) % NPHI).astype(jnp.float32)[:, None] * step
-    turn = jnp.broadcast_to(turn, (M, 128))
-    c0, s0 = weight * jnp.cos(angle), weight * jnp.sin(angle)
-    rc, rs = jnp.cos(turn), jnp.sin(turn)
-
-    slot_m = lax.dynamic_slice_in_dim(m_order, ma_index * slot_count, slot_count)
-    degree = rad_index * part_len + jnp.arange(part_len, dtype=jnp.int32)
-    keep = (degree[None, :] >= slot_m[:, None]).astype(jnp.float32)[:, None, :]
-    flip = (1 - 2 * ((slot_m[:, None] + degree[None, :]) % 2)).astype(jnp.float32)[:, None, :]
-
-    blocks = m_order.reshape(ma_count, BLOCKS, CS).transpose(1, 0, 2).reshape(BLOCKS, ma_count * CS)
-    pick = (blocks[:, :, None] == jnp.arange(M, dtype=jnp.int32)).astype(jnp.bfloat16)
-    lane = jnp.arange(16 * CS, dtype=jnp.int32)
-    row = lane[:, None]
-    owner = rad_index * ma_count + lane // CS
-    perm = (jnp.tile(selected, CS)[:, None] == owner[None, :]) & (row // SEL == lane[None, :] % CS)
-    lat = flow(spectra.reshape(channels, M, M), legendre, pick, perm.astype(jnp.bfloat16), keep, flip)
-    return dft(lat, c0, s0, rc, rs)
+    order = jnp.broadcast_to(m_order[:, None], (M, 128))
+    chosen = jnp.broadcast_to(selected[:, None], (SEL, 128))
+    lat, base = flow(spectra.reshape(2 * FIELDS, M, M), legendre, order, chosen)
+    return dft(lat, base)
 
 
 def solution(mesh):

time: 251 us -> 242 us (0.964)
  other arithmetic: 8.81 us -> 0 us
  Pallas kernels: 231 us -> 235 us
  local copies, waits for them, and re-layouts: 9.91 us -> 6 us
    convert_element_type x4 -> x0, other arithmetic: 4.04 us -> none  [the longest x1 1.72 us: local(): (blocks[:, :, None] == jnp.arange(M, dtype=jnp.int32)).astype(jnp.bfloat16)]
    mul x1 -> x0, other arithmetic: 4.01 us -> none  [local(): c0, s0 = (weight * jnp.cos(angle), weight * jnp.sin(angle))]
    pallas_call x2, Pallas kernels: 231 us -> 235 us  [the longest x1 220 us: flow(): pl.pallas_call(flow_kernel, name='flow', out_shape=[jax.ShapeDtypeStruct(...]
    unnamed x10 -> x4, local copies, waits for them, and re-layouts: 5.57 us -> 2.99 us
where the time goes in v5:
time: 242 us; the launch traced here: 241 us
  Pallas kernels  235 us (97%)
  local copies, waits for them, and re-layouts  6 us (2%)
    pallas_call x1, Pallas kernels, flow(): pl.pallas_call(flow_kernel, name='flow', out_shape=[jax.ShapeDtypeStruct(...  220 us
    pallas_call x1, Pallas kernels, dft(): pl.pallas_call(dft_kernel, name='dft', out_shape=jax.ShapeDtypeStruct((SE...  15.5 us

profile of v5, /device:TPU:1, one launch (start us, length us, event | category | flops | bytes accessed | tf_op | source)
XLA Modules:
  0.0 241.5 jit_solution(1596147908255279127)
XLA Ops:
  0.0 1.3 broadcast_in_dim.5.chosen_ref
  1.3 1.7 broadcast_in_dim.4.order_ref
  3.0 219.9 %flow.1 = (bf16[3,16,8,16,128]{4,3,2,1,0:T(8,128)(2,1)}, f32[4,1024,128]{2,1,0:T(8,128)}) custom-call(bf16[6,1024,1024]{2,1,0:T(8,128)(2,1)} %bitcast.1, bf16[64,128,512]{2,1,0:T(8,128)(2,1)} %leg_ref.1, s32[1024,128]{1,0:T(8,128)} %broadcast_in_dim.4.order_ref, s32[16,128]{1,0:T(8,128)} %broadcast_in_dim.5.chosen_ref), custom_call_target="tpu_custom_call" | custom-call | tf_op jit(solution)/shard_map/flow/pallas_call | solution.py:355
  223.0 0.0 copy-start
  223.0 1.6 copy-done
  224.5 0.0 copy-start.1
  224.6 1.4 copy-done.1
  226.0 15.5 %dft.1 = f32[16,3,2,4,3072]{4,3,2,1,0:T(4,128)} custom-call(bf16[3,16,8,16,128]{4,3,2,1,0:T(8,128)(2,1)S(1)} %copy-done.1, f32[4,1024,128]{2,1,0:T(8,128)S(1)} %copy-done), custom_call_target="tpu_custom_call" | custom-call | tf_op jit(solution)/shard_map/dft/pallas_call | solution.py:450
Async XLA Ops:
  223.0 1.6 copy-start
  224.5 1.4 copy-start.1

commit v6 on v5

--- a/solution.py
+++ b/solution.py
@@ -13,12 +13,13 @@
 BLOCKS = 4
 CS = 16
 CHUNKS = FIELDS * BLOCKS
-
-
-def flow_kernel(spec_ref, leg_ref, order_ref, chosen_ref, lat_ref, base_ref,
-                spec, leg, pick_ref, perm_ref, base, asend, arecv, coef,
+STEPS = NPHI // 2 // 256
+
+
+def flow_kernel(spec_ref, leg_ref, order_ref, chosen_ref, out_ref,
+                spec, leg, pick_ref, perm_ref, base, lat_ref, lhs, held, tiles, asend, arecv, coef,
                 part1, core1, up1, in1, part2, core2, up2, in2, latf, bsend,
-                load, leg_load, base_sem, a_s, a_r, b_s, b_r, *rad_sems):
+                load, leg_load, out_sem, a_s, a_r, b_s, b_r, *rad_sems):
     rad = lax.axis_index("rad")
     ma = lax.axis_index("ma")
     core = lax.rem(rad, 2)
@@ -61,9 +62,6 @@
                 hit = jnp.where(held == lane + 128 * n, 1.0, 0.0).astype(jnp.bfloat16)
                 pick_ref[b, pl.ds(pl.multiple_of(a * 16, 16), 16), 128 * n:128 * (n + 1)] = hit
         each(0, 16, body)
-
-    def base_copy():
-        return pltpu.make_async_copy(base, base_ref, base_sem)
 
     def make_base():
         def body(n):
@@ -78,14 +76,12 @@
                 base[where, rows, :] = scale * jnp.cos(angle)
                 base[where + 1, rows, :] = scale * jnp.sin(angle)
         each(0, 32, body)
-        base_copy().start()
 
     barrier = pltpu.get_barrier_semaphore()
     for d in (partner, up, down):
         pl.semaphore_signal(barrier, inc=1, device_id={"rad": d}, device_id_type=MESH)
     for n in range(1, 16):
         pl.semaphore_signal(barrier, inc=1, device_id={"ma": lax.rem(ma + n, 16)}, device_id_type=MESH)
-    pl.semaphore_wait(barrier, 18)
 
     def a_copy(k, n):
         to = lax.rem(ma + n, 16)
@@ -268,6 +264,87 @@
         each(0, 8, pair)
         lat_ref[f, ma] = bsend[f, ma]
 
+    def out_copy(f, u, kind):
+        tile = (2 * u, 2 * u + 1, 23 - 2 * u, 24 - 2 * u)[kind]
+        slot = 4 * lax.rem(u, 2) + kind
+        cols = pl.ds(pl.multiple_of(tile * 128, 128), 128)
+        return pltpu.make_async_copy(tiles.at[slot], out_ref.at[:, f, :, :, cols], out_sem.at[slot])
+
+    def out_wait(f, u):
+        @pl.when(u < STEPS)
+        def _():
+            for kind in range(3):
+                out_copy(f, u, kind).wait()
+
+        @pl.when(u > 0)
+        def _():
+            out_copy(f, u, 3).wait()
+
+    def make_table(u):
+        for half in range(2):
+            for g in range(2):
+                def rows(n, half=half, g=g):
+                    r = pl.ds(pl.multiple_of(512 * g + 64 * n, 64), 64)
+                    c = base[0, r, :]
+                    s = base[1, r, :]
+                    at = 256 * g + 128 * half
+                    arecv[u, pl.ds(2 * n, 2), :, :, at:at + 128] = c.reshape(2, 2, CS, 128).astype(jnp.bfloat16)
+                    arecv[u, pl.ds(2 * n, 2), :, :, 512 + at:640 + at] = (-s).reshape(2, 2, CS, 128).astype(jnp.bfloat16)
+                    rc = base[2, r, :]
+                    rs = base[3, r, :]
+                    base[0, r, :] = c * rc - s * rs
+                    base[1, r, :] = s * rc + c * rs
+                each(0, 8, rows)
+
+    left = lax.broadcasted_iota(jnp.int32, (128, 128), 1)
+    back = lax.rem(128 - left, 128)
+
+    def gather_rows(f):
+        each(1, 16, lambda n: plane_arrival(f, n).wait_recv())
+        for b in range(8):
+            x0 = lat_ref[f, 2 * b].reshape(128, 128).astype(jnp.float32)
+            x1 = lat_ref[f, 2 * b + 1].reshape(128, 128).astype(jnp.float32)
+            cols = slice(128 * b, 128 * (b + 1))
+            lhs[0, :, cols] = jnp.where(left < 64, x0, pltpu.roll(x1, 64, 1)).astype(jnp.bfloat16)
+            lhs[1, :, cols] = jnp.where(left < 64, pltpu.roll(x0, 64, 1), x1).astype(jnp.bfloat16)
+
+    def longitudes(f, u):
+        @pl.when(u >= 2)
+        def _():
+            out_wait(f, u - 2)
+        sums2 = []
+        for c in range(2):
+            acc = jnp.zeros((128, 256), jnp.float32)
+            for g in range(2):
+                at = 512 * c + 256 * g
+                table = arecv[u, :, :, :, at:at + 256].reshape(512, 256)
+                acc = acc + jnp.dot(lhs[c, :, 512 * g:512 * (g + 1)], table, preferred_element_type=jnp.float32)
+            sums2.append(acc)
+        plus = sums2[0] + sums2[1]
+        less = sums2[0] - sums2[1]
+        first, second = less[:, :128], less[:, 128:]
+        slot = 4 * lax.rem(u, 2)
+
+        def put(kind, x):
+            tiles[slot + kind] = x.reshape(SEL, 2, 4, 128)
+            out_copy(f, u, kind).start()
+
+        @pl.when(u > 0)
+        def _():
+            put(3, jnp.where(left == 0, first, held[...]))
+
+        @pl.when(u < STEPS)
+        def _():
+            put(0, plus[:, :128])
+            put(1, plus[:, 128:])
+            put(2, jnp.where(left == 0, second, jnp.take_along_axis(first, back, axis=1)))
+            held[...] = jnp.take_along_axis(second, back, axis=1)
+
+        @pl.when(u == STEPS)
+        def _():
+            out_wait(f, u - 1)
+            out_wait(f, u)
+
     def between(k, first, last, body):
         @pl.when((k >= first) & (k < last))
         def _():
@@ -278,19 +355,29 @@
             @pl.when(k >= 3)
             def _():
                 each(1, 16, lambda n: a_copy(k - 3, n).wait_send())
-            @pl.when(k < BLOCKS)
+            @pl.when((k > 0) & (k < BLOCKS))
             def _():
                 make_pick(k)
-            gather(k)
+
+            @pl.when(k > 0)
+            def _():
+                gather(k)
             each(1, 16, lambda n: a_copy(k, n).start())
             arecv[k, ma] = asend[lax.rem(k, 3), ma]
         between(k, 0, CHUNKS, send)
 
-        @pl.when(k == 6)
+        @pl.when(k == 2)
         def _():
             make_base()
         between(k, 3, CHUNKS + 3, lambda: relay.forward(k - 3))
         between(k, 4, CHUNKS + 4, lambda: sums.forward(k - 4))
+        first = jnp.where(k < 13, 2 * (k - 9), jnp.where(k == 14, 1, 4))
+        count = jnp.where((k < 9) | (k == 13), 0, jnp.where(k < 13, 1, 2))
+
+        @pl.when(k == 9)
+        def _():
+            gather_rows(0)
+        each(first, first + count, lambda u: longitudes(jnp.where(k < 13, 0, 1), u))
 
         def arrive():
             c = k - 2
@@ -324,11 +411,24 @@
                 each(1, 16, lambda n: plane_copy(f, n).start())
         between(k, 4, CHUNKS + 4, settle)
         between(k, 3, CHUNKS + 3, lambda: sums.add(k - 3))
+        between(k, 3, 3 + STEPS + 1, lambda: make_table(k - 3))
+
+        @pl.when(k == 13)
+        def _():
+            gather_rows(1)
+        second = jnp.where(k < 13, 2 * (k - 9) + 1, jnp.where(k == 13, 0, 3))
+        more = jnp.where((k < 9) | (k == 12) | (k == 15), 0, 1)
+        each(second, second + more, lambda u: longitudes(jnp.where(k < 13, 0, 1), u))
         return carry
 
+    make_pick(0)
+    gather(0)
+    pl.semaphore_wait(barrier, 18)
     lax.fori_loop(0, CHUNKS + 4, step, 0)
 
-    base_copy().wait()
+    longitudes(1, STEPS)
+    gather_rows(2)
+    each(0, STEPS + 1, lambda u: longitudes(2, u))
     relay.drain()
     sums.drain()
     for k in range(CHUNKS - 3, CHUNKS):
@@ -337,7 +437,6 @@
     def last(n):
         for f in range(FIELDS):
             plane_copy(f, n).wait_send()
-            plane_arrival(f, n).wait_recv()
     each(1, 16, last)
 
 
@@ -355,23 +454,26 @@
     return pl.pallas_call(
         flow_kernel,
         name="flow",
-        out_shape=[jax.ShapeDtypeStruct((FIELDS, 16, 8, 16, 128), bf),
-                   jax.ShapeDtypeStruct((4, M, 128), jnp.float32)],
+        out_shape=jax.ShapeDtypeStruct((SEL, FIELDS, 2, 4, NPHI), jnp.float32),
         in_specs=[hbm, hbm, vm, vm],
-        out_specs=[vm, hbm],
+        out_specs=hbm,
         scratch_shapes=[
             pltpu.VMEM((2, M, M), bf),
             pltpu.VMEM((2, CS, 128, 512), bf),
             pltpu.VMEM((BLOCKS, 16 * CS, M), bf),
             pltpu.VMEM((16 * CS, 16 * CS), bf),
             pltpu.VMEM((4, M, 128), jnp.float32),
+            pltpu.VMEM((FIELDS, 16, 8, 16, 128), bf),
+            pltpu.VMEM((2, 128, M), bf),
+            pltpu.VMEM((128, 128), jnp.float32),
+            pltpu.VMEM((8, SEL, 2, 4, 128), jnp.float32),
             pltpu.VMEM((3, 16, 2, CS, M), bf),
             pltpu.VMEM((CHUNKS, 16, 2, CS, M), bf),
             pltpu.VMEM((2, CS, SEL, 128), bf),
             *reduce_scratch, *reduce_scratch,
             pltpu.VMEM((2, 1024, 128), jnp.float32),
             pltpu.VMEM((FIELDS, 16, 8, 16, 128), bf),
-            dma((2,)), dma((2,)), dma(()),
+            dma((2,)), dma((2,)), dma((8,)),
             dma((CHUNKS, 16)), dma((CHUNKS, 16)),
             dma((FIELDS, 16)), dma((FIELDS, 16)),
             *([dma((CHUNKS,))] * 2 + [dma((CHUNKS, 2))] * 4) * 2,
@@ -381,95 +483,10 @@
     )(spec, leg, order, chosen)
 
 
-PT = 256
-STEPS = NPHI // 2 // PT
-
-
-def dft_kernel(lat_ref, base_ref, out_ref, lhs, cs, sn, ctab, stab, held):
-    low = lax.broadcasted_iota(jnp.int32, (128, 128), 1) < 64
-    for f in range(FIELDS):
-        rows = slice(128 * f, 128 * (f + 1))
-        for b in range(8):
-            x0 = lat_ref[f, 2 * b].reshape(128, 128).astype(jnp.float32)
-            x1 = lat_ref[f, 2 * b + 1].reshape(128, 128).astype(jnp.float32)
-            cols = slice(128 * b, 128 * (b + 1))
-            lhs[0, rows, cols] = jnp.where(low, x0, pltpu.roll(x1, 64, 1)).astype(jnp.bfloat16)
-            lhs[1, rows, cols] = jnp.where(low, pltpu.roll(x0, 64, 1), x1).astype(jnp.bfloat16)
-    cs[...] = base_ref[0]
-    sn[...] = base_ref[1]
-    lane = lax.broadcasted_iota(jnp.int32, (128, 128), 1)
-    back = lax.rem(128 - lane, 128)
-
-    def put(f, tile, x):
-        cols = pl.ds(pl.multiple_of(tile * 128, 128), 128)
-        out_ref[:, f, :, :, cols] = x.reshape(SEL, 2, 4, 128)
-
-    def step(u, carry):
-        for half in range(2):
-            cols = slice(128 * half, 128 * (half + 1))
-
-            def rows(b, carry, cols=cols):
-                r = pl.ds(pl.multiple_of(b * 64, 64), 64)
-                c = cs[r]
-                s = sn[r]
-                ctab[r, cols] = c.astype(jnp.bfloat16)
-                stab[r, cols] = (-s).astype(jnp.bfloat16)
-                rc = base_ref[2, r]
-                rs = base_ref[3, r]
-                cs[r] = c * rc - s * rs
-                sn[r] = s * rc + c * rs
-                return carry
-            lax.fori_loop(0, 16, rows, 0)
-        for f in range(FIELDS):
-            at = slice(128 * f, 128 * (f + 1))
-            even = jnp.dot(lhs[0, at], ctab[...], preferred_element_type=jnp.float32)
-            odd = jnp.dot(lhs[1, at], stab[...], preferred_element_type=jnp.float32)
-            plus = even + odd
-            less = even - odd
-            first, second = less[:, :128], less[:, 128:]
-
-            @pl.when(u > 0)
-            def _():
-                put(f, 24 - 2 * u, jnp.where(lane == 0, first, held[f]))
-
-            @pl.when(u < STEPS)
-            def _():
-                put(f, 2 * u, plus[:, :128])
-                put(f, 2 * u + 1, plus[:, 128:])
-                turned = jnp.take_along_axis(first, back, axis=1)
-                put(f, 23 - 2 * u, jnp.where(lane == 0, second, turned))
-                held[f] = jnp.take_along_axis(second, back, axis=1)
-        return carry
-
-    lax.fori_loop(0, STEPS + 1, step, 0)
-
-
-def dft(lat, base):
-    vm = pl.BlockSpec(memory_space=pltpu.VMEM)
-    f32 = jnp.float32
-    return pl.pallas_call(
-        dft_kernel,
-        name="dft",
-        out_shape=jax.ShapeDtypeStruct((SEL, FIELDS, 2, 4, NPHI), f32),
-        in_specs=[vm, vm],
-        out_specs=vm,
-        scratch_shapes=[
-            pltpu.VMEM((2, FIELDS * 128, M), jnp.bfloat16),
-            pltpu.VMEM((M, 128), f32),
-            pltpu.VMEM((M, 128), f32),
-            pltpu.VMEM((M, PT), jnp.bfloat16),
-            pltpu.VMEM((M, PT), jnp.bfloat16),
-            pltpu.VMEM((FIELDS, 128, 128), f32),
-        ],
-        compiler_params=pltpu.CompilerParams(vmem_limit_bytes=48 * 1024 * 1024),
-    )(lat, base)
-
-
 def local(spectra, legendre, selected, m_order):
     order = jnp.broadcast_to(m_order[:, None], (M, 128))
     chosen = jnp.broadcast_to(selected[:, None], (SEL, 128))
-    lat, base = flow(spectra.reshape(2 * FIELDS, M, M), legendre, order, chosen)
-    return dft(lat, base)
+    return flow(spectra.reshape(2 * FIELDS, M, M), legendre, order, chosen)
 
 
 def solution(mesh):

time: 242 us -> 230 us (0.950)
  Pallas kernels: 235 us -> 221 us
    pallas_call x2 -> x1, Pallas kernels: 235 us -> 221 us  [flow(): pl.pallas_call(flow_kernel, name='flow', out_shape=jax.ShapeDtypeStruct((...]
    unnamed x4 -> x1, local copies, waits for them, and re-layouts: 2.99 us -> 5.11 us
where the time goes in v6:
time: 230 us; the launch traced here: 229 us
  Pallas kernels  221 us (96%)
  local copies, waits for them, and re-layouts  8.11 us (4%)
    pallas_call x1, Pallas kernels, flow(): pl.pallas_call(flow_kernel, name='flow', out_shape=jax.ShapeDtypeStruct((...  221 us
    unnamed x1, local copies, waits for them, and re-layouts  5.11 us

profile of v6, /device:TPU:1, one launch (start us, length us, event | category | flops | bytes accessed | tf_op | source)
XLA Modules:
  0.0 228.9 jit_solution(12043496491652431717)
XLA Ops:
  0.0 1.3 broadcast_in_dim.5.chosen_ref
  1.3 1.7 broadcast_in_dim.4.order_ref
  3.0 220.7 %flow.1 = f32[16,3,2,4,3072]{4,3,2,1,0:T(4,128)} custom-call(bf16[6,1024,1024]{2,1,0:T(8,128)(2,1)} %bitcast.1, bf16[64,128,512]{2,1,0:T(8,128)(2,1)} %leg_ref.1, s32[1024,128]{1,0:T(8,128)} %broadcast_in_dim.4.order_ref, s32[16,128]{1,0:T(8,128)} %broadcast_in_dim.5.chosen_ref), custom_call_target="tpu_custom_call" | custom-call | tf_op jit(solution)/shard_map/flow/pallas_call | solution.py:454
  223.7 5.1 %copy.6 = f32[16,3,2,4,3072]{4,3,2,1,0:T(4,128)} copy(f32[16,3,2,4,3072]{4,3,2,1,0:T(4,128)} %flow.1) | data formatting | bytes 9437184

commit v7 on v6

--- a/solution.py
+++ b/solution.py
@@ -16,10 +16,78 @@
 STEPS = NPHI // 2 // 256
 
 
-def flow_kernel(spec_ref, leg_ref, order_ref, chosen_ref, out_ref,
-                spec, leg, pick_ref, perm_ref, base, lat_ref, lhs, held, tiles, asend, arecv, coef,
+def tile_copy(tiles, sems, target, u, kind):
+    tile = (2 * u, 2 * u + 1, 23 - 2 * u, 24 - 2 * u)[kind]
+    slot = 4 * lax.rem(u, 2) + kind
+    cols = pl.ds(pl.multiple_of(tile * 128, 128), 128)
+    return pltpu.make_async_copy(tiles.at[slot], target(cols), sems.at[slot])
+
+
+def spread_rows(lat, lhs):
+    low = lax.broadcasted_iota(jnp.int32, (128, 128), 1) < 64
+    for b in range(8):
+        x0 = lat(2 * b).reshape(128, 128).astype(jnp.float32)
+        x1 = lat(2 * b + 1).reshape(128, 128).astype(jnp.float32)
+        cols = slice(128 * b, 128 * (b + 1))
+        lhs[0, :, cols] = jnp.where(low, x0, pltpu.roll(x1, 64, 1)).astype(jnp.bfloat16)
+        lhs[1, :, cols] = jnp.where(low, pltpu.roll(x0, 64, 1), x1).astype(jnp.bfloat16)
+
+
+def longitude_step(u, table, lhs, held, tiles, out_copy):
+    lane = lax.broadcasted_iota(jnp.int32, (128, 128), 1)
+    back = lax.rem(128 - lane, 128)
+
+    def out_wait(v):
+        @pl.when(v < STEPS)
+        def _():
+            for kind in range(3):
+                out_copy(v, kind).wait()
+
+        @pl.when(v > 0)
+        def _():
+            out_copy(v, 3).wait()
+
+    @pl.when(u >= 2)
+    def _():
+        out_wait(u - 2)
+    parts = []
+    for c in range(2):
+        acc = jnp.zeros((128, 256), jnp.float32)
+        for g in range(2):
+            at = 512 * c + 256 * g
+            rows = table(slice(at, at + 256)).reshape(512, 256)
+            acc = acc + jnp.dot(lhs[c, :, 512 * g:512 * (g + 1)], rows, preferred_element_type=jnp.float32)
+        parts.append(acc)
+    plus = parts[0] + parts[1]
+    less = parts[0] - parts[1]
+    first, second = less[:, :128], less[:, 128:]
+    slot = 4 * lax.rem(u, 2)
+
+    def put(kind, x):
+        tiles[slot + kind] = x.reshape(SEL, 2, 4, 128)
+        out_copy(u, kind).start()
+
+    @pl.when(u > 0)
+    def _():
+        put(3, jnp.where(lane == 0, first, held[...]))
+
+    @pl.when(u < STEPS)
+    def _():
+        put(0, plus[:, :128])
+        put(1, plus[:, 128:])
+        put(2, jnp.where(lane == 0, second, jnp.take_along_axis(first, back, axis=1)))
+        held[...] = jnp.take_along_axis(second, back, axis=1)
+
+    @pl.when(u == STEPS)
+    def _():
+        out_wait(u - 1)
+        out_wait(u)
+
+
+def flow_kernel(spec_ref, leg_ref, held_ref, selected_ref, out_ref, last_ref, table_ref,
+                spec, leg, order_ref, pick_ref, perm_ref, base, lat_ref, lhs, held, tiles, asend, arecv, coef,
                 part1, core1, up1, in1, part2, core2, up2, in2, latf, bsend,
-                load, leg_load, out_sem, a_s, a_r, b_s, b_r, *rad_sems):
+                load, leg_load, out_sem, table_sem, last_sem, a_s, a_r, b_s, b_r, *rad_sems):
     rad = lax.axis_index("rad")
     ma = lax.axis_index("ma")
     core = lax.rem(rad, 2)
@@ -50,9 +118,16 @@
 
     lane = lax.broadcasted_iota(jnp.int32, (16, 128), 1)
     degree = rad * 128 + lax.broadcasted_iota(jnp.int32, (1, 128), 1)
+    for r in range(8):
+        line = jnp.broadcast_to(held_ref[r:r + 1, :].astype(jnp.float32), (128, 128))
+        order_ref[128 * r:128 * (r + 1), :] = line.T.astype(jnp.int32)
+    row = lax.broadcasted_iota(jnp.int32, (16, 128), 0)
+    chosen = jnp.zeros((16, 128), jnp.int32)
+    for i in range(SEL):
+        chosen = jnp.where(row == i, selected_ref[i], chosen)
     for j in range(CS):
         for half in range(2):
-            hit = (chosen_ref[...] == rad * 16 + 8 * half + lane // 16) & (lax.rem(lane, 16) == j)
+            hit = (chosen == rad * 16 + 8 * half + lane // 16) & (lax.rem(lane, 16) == j)
             perm_ref[16 * j:16 * (j + 1), 128 * half:128 * (half + 1)] = jnp.where(hit, 1.0, 0.0).astype(jnp.bfloat16)
 
     def make_pick(b):
@@ -264,22 +339,6 @@
         each(0, 8, pair)
         lat_ref[f, ma] = bsend[f, ma]
 
-    def out_copy(f, u, kind):
-        tile = (2 * u, 2 * u + 1, 23 - 2 * u, 24 - 2 * u)[kind]
-        slot = 4 * lax.rem(u, 2) + kind
-        cols = pl.ds(pl.multiple_of(tile * 128, 128), 128)
-        return pltpu.make_async_copy(tiles.at[slot], out_ref.at[:, f, :, :, cols], out_sem.at[slot])
-
-    def out_wait(f, u):
-        @pl.when(u < STEPS)
-        def _():
-            for kind in range(3):
-                out_copy(f, u, kind).wait()
-
-        @pl.when(u > 0)
-        def _():
-            out_copy(f, u, 3).wait()
-
     def make_table(u):
         for half in range(2):
             for g in range(2):
@@ -296,54 +355,19 @@
                     base[1, r, :] = s * rc + c * rs
                 each(0, 8, rows)
 
-    left = lax.broadcasted_iota(jnp.int32, (128, 128), 1)
-    back = lax.rem(128 - left, 128)
+    def out_copy(f, u, kind):
+        return tile_copy(tiles, out_sem, lambda cols: out_ref.at[:, f, :, :, cols], u, kind)
+
+    def table_copy(u):
+        return pltpu.make_async_copy(arecv.at[u], table_ref.at[u], table_sem.at[u])
 
     def gather_rows(f):
         each(1, 16, lambda n: plane_arrival(f, n).wait_recv())
-        for b in range(8):
-            x0 = lat_ref[f, 2 * b].reshape(128, 128).astype(jnp.float32)
-            x1 = lat_ref[f, 2 * b + 1].reshape(128, 128).astype(jnp.float32)
-            cols = slice(128 * b, 128 * (b + 1))
-            lhs[0, :, cols] = jnp.where(left < 64, x0, pltpu.roll(x1, 64, 1)).astype(jnp.bfloat16)
-            lhs[1, :, cols] = jnp.where(left < 64, pltpu.roll(x0, 64, 1), x1).astype(jnp.bfloat16)
+        spread_rows(lambda a: lat_ref[f, a], lhs)
 
     def longitudes(f, u):
-        @pl.when(u >= 2)
-        def _():
-            out_wait(f, u - 2)
-        sums2 = []
-        for c in range(2):
-            acc = jnp.zeros((128, 256), jnp.float32)
-            for g in range(2):
-                at = 512 * c + 256 * g
-                table = arecv[u, :, :, :, at:at + 256].reshape(512, 256)
-                acc = acc + jnp.dot(lhs[c, :, 512 * g:512 * (g + 1)], table, preferred_element_type=jnp.float32)
-            sums2.append(acc)
-        plus = sums2[0] + sums2[1]
-        less = sums2[0] - sums2[1]
-        first, second = less[:, :128], less[:, 128:]
-        slot = 4 * lax.rem(u, 2)
-
-        def put(kind, x):
-            tiles[slot + kind] = x.reshape(SEL, 2, 4, 128)
-            out_copy(f, u, kind).start()
-
-        @pl.when(u > 0)
-        def _():
-            put(3, jnp.where(left == 0, first, held[...]))
-
-        @pl.when(u < STEPS)
-        def _():
-            put(0, plus[:, :128])
-            put(1, plus[:, 128:])
-            put(2, jnp.where(left == 0, second, jnp.take_along_axis(first, back, axis=1)))
-            held[...] = jnp.take_along_axis(second, back, axis=1)
-
-        @pl.when(u == STEPS)
-        def _():
-            out_wait(f, u - 1)
-            out_wait(f, u)
+        longitude_step(u, lambda cols: arecv[u, :, :, :, cols], lhs, held, tiles,
+                       lambda v, kind: out_copy(f, v, kind))
 
     def between(k, first, last, body):
         @pl.when((k >= first) & (k < last))
@@ -411,7 +435,11 @@
                 each(1, 16, lambda n: plane_copy(f, n).start())
         between(k, 4, CHUNKS + 4, settle)
         between(k, 3, CHUNKS + 3, lambda: sums.add(k - 3))
-        between(k, 3, 3 + STEPS + 1, lambda: make_table(k - 3))
+
+        def fill():
+            make_table(k - 3)
+            table_copy(k - 3).start()
+        between(k, 3, 3 + STEPS + 1, fill)
 
         @pl.when(k == 13)
         def _():
@@ -427,8 +455,11 @@
     lax.fori_loop(0, CHUNKS + 4, step, 0)
 
     longitudes(1, STEPS)
-    gather_rows(2)
-    each(0, STEPS + 1, lambda u: longitudes(2, u))
+    each(1, 16, lambda n: plane_arrival(2, n).wait_recv())
+    last_copy = pltpu.make_async_copy(lat_ref.at[2], last_ref, last_sem)
+    last_copy.start()
+    last_copy.wait()
+    each(0, STEPS + 1, lambda u: table_copy(u).wait())
     relay.drain()
     sums.drain()
     for k in range(CHUNKS - 3, CHUNKS):
@@ -454,12 +485,15 @@
     return pl.pallas_call(
         flow_kernel,
         name="flow",
-        out_shape=jax.ShapeDtypeStruct((SEL, FIELDS, 2, 4, NPHI), jnp.float32),
-        in_specs=[hbm, hbm, vm, vm],
-        out_specs=hbm,
+        out_shape=[jax.ShapeDtypeStruct((SEL, FIELDS - 1, 2, 4, NPHI), jnp.float32),
+                   jax.ShapeDtypeStruct((16, 8, 16, 128), bf),
+                   jax.ShapeDtypeStruct((STEPS + 1, 16, 2, CS, M), bf)],
+        in_specs=[hbm, hbm, vm, pl.BlockSpec(memory_space=pltpu.SMEM)],
+        out_specs=[hbm, hbm, hbm],
         scratch_shapes=[
             pltpu.VMEM((2, M, M), bf),
             pltpu.VMEM((2, CS, 128, 512), bf),
+            pltpu.VMEM((M, 128), jnp.int32),
             pltpu.VMEM((BLOCKS, 16 * CS, M), bf),
             pltpu.VMEM((16 * CS, 16 * CS), bf),
             pltpu.VMEM((4, M, 128), jnp.float32),
@@ -473,7 +507,7 @@
             *reduce_scratch, *reduce_scratch,
             pltpu.VMEM((2, 1024, 128), jnp.float32),
             pltpu.VMEM((FIELDS, 16, 8, 16, 128), bf),
-            dma((2,)), dma((2,)), dma((8,)),
+            dma((2,)), dma((2,)), dma((8,)), dma((STEPS + 1,)), dma(()),
             dma((CHUNKS, 16)), dma((CHUNKS, 16)),
             dma((FIELDS, 16)), dma((FIELDS, 16)),
             *([dma((CHUNKS,))] * 2 + [dma((CHUNKS, 2))] * 4) * 2,
@@ -483,10 +517,62 @@
     )(spec, leg, order, chosen)
 
 
+def last_kernel(done_ref, lat_ref, table_ref, out_ref, moved, tables, lhs, held, tiles, in_sem, back_sem, table_sem, out_sem):
+    def move_in(n):
+        return pltpu.make_async_copy(done_ref.at[pl.ds(4 * n, 4)], moved.at[pl.ds(4 * n, 4)], in_sem.at[n])
+
+    def move_out(n):
+        return pltpu.make_async_copy(moved.at[pl.ds(4 * n, 4)], out_ref.at[pl.ds(4 * n, 4), :2], back_sem.at[n])
+
+    def table_copy(u):
+        return pltpu.make_async_copy(table_ref.at[u], tables.at[u], table_sem.at[u])
+
+    table_copy(0).start()
+    for u in range(1, STEPS + 1):
+        if u <= 4:
+            move_in(u - 1).start()
+        table_copy(u).start()
+    spread_rows(lambda a: lat_ref[a], lhs)
+
+    def step(u, carry):
+        table_copy(u).wait()
+
+        @pl.when((u >= 1) & (u < 5))
+        def _():
+            move_in(u - 1).wait()
+            move_out(u - 1).start()
+        longitude_step(u, lambda cols: tables[u, :, :, :, cols], lhs, held, tiles,
+                       lambda v, kind: tile_copy(tiles, out_sem, lambda c: out_ref.at[:, 2, :, :, c], v, kind))
+        return carry
+    lax.fori_loop(0, STEPS + 1, step, 0)
+    for n in range(4):
+        move_out(n).wait()
+
+
+def last(done, lat, tables):
+    bf = jnp.bfloat16
+    hbm = pl.BlockSpec(memory_space=pl.ANY)
+    dma = pltpu.SemaphoreType.DMA
+    return pl.pallas_call(
+        last_kernel,
+        name="last",
+        out_shape=jax.ShapeDtypeStruct((SEL, FIELDS, 2, 4, NPHI), jnp.float32),
+        in_specs=[hbm, pl.BlockSpec(memory_space=pltpu.VMEM), hbm],
+        out_specs=hbm,
+        scratch_shapes=[
+            pltpu.VMEM((SEL, FIELDS - 1, 2, 4, NPHI), jnp.float32),
+            pltpu.VMEM((STEPS + 1, 16, 2, CS, M), bf),
+            pltpu.VMEM((2, 128, M), bf),
+            pltpu.VMEM((128, 128), jnp.float32),
+            pltpu.VMEM((8, SEL, 2, 4, 128), jnp.float32),
+            dma((4,)), dma((4,)), dma((STEPS + 1,)), dma((8,)),
+        ],
+        compiler_params=pltpu.CompilerParams(vmem_limit_bytes=60 * 1024 * 1024),
+    )(done, lat, tables)
+
+
 def local(spectra, legendre, selected, m_order):
-    order = jnp.broadcast_to(m_order[:, None], (M, 128))
-    chosen = jnp.broadcast_to(selected[:, None], (SEL, 128))
-    return flow(spectra.reshape(2 * FIELDS, M, M), legendre, order, chosen)
+    return last(*flow(spectra.reshape(2 * FIELDS, M, M), legendre, m_order.reshape(8, 128), selected))
 
 
 def solution(mesh):

time: 230 us -> 225 us (0.978)
  local copies, waits for them, and re-layouts: 8.11 us -> 0 us
  Pallas kernels: 221 us -> 224 us
    unnamed x1 -> x0, local copies, waits for them, and re-layouts: 5.11 us -> none
    pallas_call x1 -> x2, Pallas kernels: 221 us -> 224 us  [the longest x1 216 us: flow(): pl.pallas_call(flow_kernel, name='flow', out_shape=[jax.ShapeDtypeStruct(...]
    broadcast_in_dim x2 -> x0, local copies, waits for them, and re-layouts: 3 us -> none  [the longest x1 1.68 us: local(): order = jnp.broadcast_to(m_order[:, None], (M, 128))]
where the time goes in v7:
time: 225 us; the launch traced here: 224 us
  Pallas kernels  224 us (100%)
    pallas_call x1, Pallas kernels, flow(): pl.pallas_call(flow_kernel, name='flow', out_shape=[jax.ShapeDtypeStruct(...  216 us
    pallas_call x1, Pallas kernels, last(): pl.pallas_call(last_kernel, name='last', out_shape=jax.ShapeDtypeStruct((...  7.53 us

profile of v7, /device:TPU:1, one launch (start us, length us, event | category | flops | bytes accessed | tf_op | source)
XLA Modules:
  0.0 223.9 jit_solution(5745361863838298188)
XLA Ops:
  0.0 216.4 %flow.1 = (f32[16,2,2,4,3072]{4,3,2,1,0:T(4,128)}, bf16[16,8,16,128]{3,2,1,0:T(8,128)(2,1)}, bf16[7,16,2,16,1024]{4,3,2,1,0:T(8,128)(2,1)}) custom-call(bf16[6,1024,1024]{2,1,0:T(8,128)(2,1)} %bitcast.2, bf16[64,128,512]{2,1,0:T(8,128)(2,1)} %leg_ref.1, s32[8,128]{1,0:T(8,128)} %bitcast.3, s32[16]{0:T(128)} %selected_ref.1), custom_call_target="tpu_custom_call" | custom-call | tf_op jit(solution)/shard_map/flow/pallas_call | solution.py:485
  216.4 7.5 %last.1 = f32[16,3,2,4,3072]{4,3,2,1,0:T(4,128)} custom-call(f32[16,2,2,4,3072]{4,3,2,1,0:T(4,128)} %get-tuple-element.8.done_ref, bf16[16,8,16,128]{3,2,1,0:T(8,128)(2,1)} %get-tuple-element.9.lat_ref, bf16[7,16,2,16,1024]{4,3,2,1,0:T(8,128)(2,1)} %get-tuple-element.10.table_ref), custom_call_target="tpu_custom_call" | custom-call | tf_op jit(solution)/shard_map/last/pallas_call | solution.py:556

commit v8 on v7

--- a/solution.py
+++ b/solution.py
@@ -14,6 +14,7 @@
 CS = 16
 CHUNKS = FIELDS * BLOCKS
 STEPS = NPHI // 2 // 256
+HALVES = 2 * FIELDS
 
 
 def tile_copy(tiles, sems, target, u, kind):
@@ -24,13 +25,20 @@
 
 
 def spread_rows(lat, lhs):
-    low = lax.broadcasted_iota(jnp.int32, (128, 128), 1) < 64
+    quarter = lax.broadcasted_iota(jnp.int32, (64, 128), 1) // 32
     for b in range(8):
-        x0 = lat(2 * b).reshape(128, 128).astype(jnp.float32)
-        x1 = lat(2 * b + 1).reshape(128, 128).astype(jnp.float32)
-        cols = slice(128 * b, 128 * (b + 1))
-        lhs[0, :, cols] = jnp.where(low, x0, pltpu.roll(x1, 64, 1)).astype(jnp.bfloat16)
-        lhs[1, :, cols] = jnp.where(low, pltpu.roll(x0, 64, 1), x1).astype(jnp.bfloat16)
+        held = [lat(n % 2, 2 * b + n // 2).reshape(64, 128).astype(jnp.float32) for n in range(4)]
+        for c in range(2):
+            pair = []
+            for odd in range(2):
+                row = None
+                for n in range(4):
+                    shift = (32 * n - 64 * odd - 32 * c) % 128
+                    piece = pltpu.roll(held[n], shift, 1) if shift else held[n]
+                    row = piece if row is None else jnp.where(quarter == n, piece, row)
+                pair.append(row)
+            rows = [pair[n % 2][8 * (n // 2):8 * (n // 2) + 8] for n in range(16)]
+            lhs[c, :, 128 * b:128 * (b + 1)] = jnp.concatenate(rows, axis=0).astype(jnp.bfloat16)
 
 
 def longitude_step(u, table, lhs, held, tiles, out_copy):
@@ -321,23 +329,23 @@
                     part2[1, ring, q, side, j] = odd[16 * side:16 * (side + 1)]
         each(0, CS, slot)
 
-    def turn(f):
-        def pair(n):
-            halves = []
-            for i in (2 * n, 2 * n + 1):
+    def turn(half):
+        def quad(n):
+            turned = []
+            for i in (4 * n, 4 * n + 2):
                 block = jnp.concatenate(
-                    [latf[c, pl.ds(i, 64, stride=16), :] for c in range(2)], axis=0)
-                halves.append(block.T)
+                    [latf[c, pl.ds(i + odd, 32, stride=16), :] for odd in range(2) for c in range(2)], axis=0)
+                turned.append(block.T)
             for b in range(8):
                 first, second = [], []
-                for x in halves:
+                for x in turned:
                     nt, st = x[8 * b:8 * b + 8], x[64 + 8 * b:64 + 8 * b + 8]
                     first.append(jnp.where(top, nt, pltpu.roll(st, 4, 0)))
                     second.append(jnp.where(top, pltpu.roll(nt, 4, 0), st))
-                bsend[f, 2 * b, n] = jnp.concatenate(first, axis=0).astype(jnp.bfloat16)
-                bsend[f, 2 * b + 1, n] = jnp.concatenate(second, axis=0).astype(jnp.bfloat16)
-        each(0, 8, pair)
-        lat_ref[f, ma] = bsend[f, ma]
+                bsend[half, 2 * b, n] = jnp.concatenate(first, axis=0).astype(jnp.bfloat16)
+                bsend[half, 2 * b + 1, n] = jnp.concatenate(second, axis=0).astype(jnp.bfloat16)
+        each(0, 4, quad)
+        lat_ref[half, ma] = bsend[half, ma]
 
     def make_table(u):
         for half in range(2):
@@ -362,8 +370,9 @@
         return pltpu.make_async_copy(arecv.at[u], table_ref.at[u], table_sem.at[u])
 
     def gather_rows(f):
-        each(1, 16, lambda n: plane_arrival(f, n).wait_recv())
-        spread_rows(lambda a: lat_ref[f, a], lhs)
+        for half in range(2):
+            each(1, 16, lambda n: plane_arrival(2 * f + half, n).wait_recv())
+        spread_rows(lambda half, a: lat_ref[2 * f + half, a], lhs)
 
     def longitudes(f, u):
         longitude_step(u, lambda cols: arecv[u, :, :, :, cols], lhs, held, tiles,
@@ -394,14 +403,14 @@
         def _():
             make_base()
         between(k, 3, CHUNKS + 3, lambda: relay.forward(k - 3))
-        between(k, 4, CHUNKS + 4, lambda: sums.forward(k - 4))
-        first = jnp.where(k < 13, 2 * (k - 9), jnp.where(k == 14, 1, 4))
-        count = jnp.where((k < 9) | (k == 13), 0, jnp.where(k < 13, 1, 2))
-
-        @pl.when(k == 9)
+        between(k, 5, CHUNKS + 5, lambda: sums.forward(k - 5))
+        first = jnp.where(k < 14, 2 * (k - 10), jnp.where(k == 15, 1, 4))
+        count = jnp.where((k < 10) | (k == 14), 0, jnp.where(k < 14, 1, 2))
+
+        @pl.when(k == 10)
         def _():
             gather_rows(0)
-        each(first, first + count, lambda u: longitudes(jnp.where(k < 13, 0, 1), u))
+        each(first, first + count, lambda u: longitudes(jnp.where(k < 14, 0, 1), u))
 
         def arrive():
             c = k - 2
@@ -412,51 +421,51 @@
         between(k, 2, CHUNKS + 2, arrive)
 
         def transform():
-            c = k - 3
+            c = k - 4
             sums.free(c)
             legendre(c)
             sums.core_copy(c).start()
-        between(k, 3, CHUNKS + 3, transform)
+        between(k, 4, CHUNKS + 4, transform)
         between(k, 2, CHUNKS + 2, lambda: relay.add(k - 2))
 
         def settle():
-            c = k - 4
-            f = c // BLOCKS
-            block = lax.rem(c, BLOCKS)
-            rows = pl.ds(pl.multiple_of(block * 256, 256), 256)
+            c = k - 5
+            half = c // 2
+            rows = pl.ds(pl.multiple_of(lax.rem(c, 2) * 256, 256), 256)
 
             def store(side, total):
                 latf[side, rows, :] = total.reshape(256, 128)
             sums.finish(c, store)
 
-            @pl.when(block == BLOCKS - 1)
+            @pl.when(lax.rem(c, 2) == 1)
             def _():
-                turn(f)
-                each(1, 16, lambda n: plane_copy(f, n).start())
-        between(k, 4, CHUNKS + 4, settle)
-        between(k, 3, CHUNKS + 3, lambda: sums.add(k - 3))
+                turn(half)
+                each(1, 16, lambda n: plane_copy(half, n).start())
+        between(k, 5, CHUNKS + 5, settle)
+        between(k, 4, CHUNKS + 4, lambda: sums.add(k - 4))
 
         def fill():
             make_table(k - 3)
             table_copy(k - 3).start()
         between(k, 3, 3 + STEPS + 1, fill)
 
-        @pl.when(k == 13)
+        @pl.when(k == 14)
         def _():
             gather_rows(1)
-        second = jnp.where(k < 13, 2 * (k - 9) + 1, jnp.where(k == 13, 0, 3))
-        more = jnp.where((k < 9) | (k == 12) | (k == 15), 0, 1)
-        each(second, second + more, lambda u: longitudes(jnp.where(k < 13, 0, 1), u))
+        second = jnp.where(k < 14, 2 * (k - 10) + 1, jnp.where(k == 14, 0, 3))
+        more = jnp.where((k < 10) | (k == 13) | (k == 16), 0, 1)
+        each(second, second + more, lambda u: longitudes(jnp.where(k < 14, 0, 1), u))
         return carry
 
     make_pick(0)
     gather(0)
     pl.semaphore_wait(barrier, 18)
-    lax.fori_loop(0, CHUNKS + 4, step, 0)
+    lax.fori_loop(0, CHUNKS + 5, step, 0)
 
     longitudes(1, STEPS)
-    each(1, 16, lambda n: plane_arrival(2, n).wait_recv())
-    last_copy = pltpu.make_async_copy(lat_ref.at[2], last_ref, last_sem)
+    for half in (HALVES - 2, HALVES - 1):
+        each(1, 16, lambda n: plane_arrival(half, n).wait_recv())
+    last_copy = pltpu.make_async_copy(lat_ref.at[pl.ds(HALVES - 2, 2)], last_ref, last_sem)
     last_copy.start()
     last_copy.wait()
     each(0, STEPS + 1, lambda u: table_copy(u).wait())
@@ -466,8 +475,8 @@
         each(1, 16, lambda n: a_copy(k, n).wait_send())
 
     def last(n):
-        for f in range(FIELDS):
-            plane_copy(f, n).wait_send()
+        for half in range(HALVES):
+            plane_copy(half, n).wait_send()
     each(1, 16, last)
 
 
@@ -486,7 +495,7 @@
         flow_kernel,
         name="flow",
         out_shape=[jax.ShapeDtypeStruct((SEL, FIELDS - 1, 2, 4, NPHI), jnp.float32),
-                   jax.ShapeDtypeStruct((16, 8, 16, 128), bf),
+                   jax.ShapeDtypeStruct((2, 16, 4, 16, 128), bf),
                    jax.ShapeDtypeStruct((STEPS + 1, 16, 2, CS, M), bf)],
         in_specs=[hbm, hbm, vm, pl.BlockSpec(memory_space=pltpu.SMEM)],
         out_specs=[hbm, hbm, hbm],
@@ -497,7 +506,7 @@
             pltpu.VMEM((BLOCKS, 16 * CS, M), bf),
             pltpu.VMEM((16 * CS, 16 * CS), bf),
             pltpu.VMEM((4, M, 128), jnp.float32),
-            pltpu.VMEM((FIELDS, 16, 8, 16, 128), bf),
+            pltpu.VMEM((HALVES, 16, 4, 16, 128), bf),
             pltpu.VMEM((2, 128, M), bf),
             pltpu.VMEM((128, 128), jnp.float32),
             pltpu.VMEM((8, SEL, 2, 4, 128), jnp.float32),
@@ -505,11 +514,11 @@
             pltpu.VMEM((CHUNKS, 16, 2, CS, M), bf),
             pltpu.VMEM((2, CS, SEL, 128), bf),
             *reduce_scratch, *reduce_scratch,
-            pltpu.VMEM((2, 1024, 128), jnp.float32),
-            pltpu.VMEM((FIELDS, 16, 8, 16, 128), bf),
+            pltpu.VMEM((2, 512, 128), jnp.float32),
+            pltpu.VMEM((HALVES, 16, 4, 16, 128), bf),
             dma((2,)), dma((2,)), dma((8,)), dma((STEPS + 1,)), dma(()),
             dma((CHUNKS, 16)), dma((CHUNKS, 16)),
-            dma((FIELDS, 16)), dma((FIELDS, 16)),
+            dma((HALVES, 16)), dma((HALVES, 16)),
             *([dma((CHUNKS,))] * 2 + [dma((CHUNKS, 2))] * 4) * 2,
         ],
         compiler_params=pltpu.CompilerParams(
@@ -532,7 +541,7 @@
         if u <= 4:
             move_in(u - 1).start()
         table_copy(u).start()
-    spread_rows(lambda a: lat_ref[a], lhs)
+    spread_rows(lambda half, a: lat_ref[half, a], lhs)
 
     def step(u, carry):
         table_copy(u).wait()

time: 225 us -> 218 us (0.969)
  Pallas kernels: 224 us -> 217 us
    pallas_call x1, Pallas kernels: 216 us -> 209 us  [flow(): pl.pallas_call(flow_kernel, name='flow', out_shape=[jax.ShapeDtypeStruct(...]
where the time goes in v8:
time: 218 us; the launch traced here: 217 us
  Pallas kernels  217 us (100%)
    pallas_call x1, Pallas kernels, flow(): pl.pallas_call(flow_kernel, name='flow', out_shape=[jax.ShapeDtypeStruct(...  209 us
    pallas_call x1, Pallas kernels, last(): pl.pallas_call(last_kernel, name='last', out_shape=jax.ShapeDtypeStruct((...  8.08 us

profile of v8, /device:TPU:1, one launch (start us, length us, event | category | flops | bytes accessed | tf_op | source)
XLA Modules:
  0.0 217.5 jit_solution(5460767501137978612)
XLA Ops:
  0.0 209.4 %flow.1 = (f32[16,2,2,4,3072]{4,3,2,1,0:T(4,128)}, bf16[2,16,4,16,128]{4,3,2,1,0:T(8,128)(2,1)}, bf16[7,16,2,16,1024]{4,3,2,1,0:T(8,128)(2,1)}) custom-call(bf16[6,1024,1024]{2,1,0:T(8,128)(2,1)} %bitcast.2, bf16[64,128,512]{2,1,0:T(8,128)(2,1)} %leg_ref.1, s32[8,128]{1,0:T(8,128)} %bitcast.3, s32[16]{0:T(128)} %selected_ref.1), custom_call_target="tpu_custom_call" | custom-call | tf_op jit(solution)/shard_map/flow/pallas_call | solution.py:494
  209.4 8.1 %last.1 = f32[16,3,2,4,3072]{4,3,2,1,0:T(4,128)} custom-call(f32[16,2,2,4,3072]{4,3,2,1,0:T(4,128)} %get-tuple-element.8.done_ref, bf16[2,16,4,16,128]{4,3,2,1,0:T(8,128)(2,1)} %get-tuple-element.9.lat_ref, bf16[7,16,2,16,1024]{4,3,2,1,0:T(8,128)(2,1)} %get-tuple-element.10.table_ref), custom_call_target="tpu_custom_call" | custom-call | tf_op jit(solution)/shard_map/last/pallas_call | solution.py:565

commit v9 on v8

--- a/solution.py
+++ b/solution.py
@@ -405,7 +405,7 @@
         between(k, 3, CHUNKS + 3, lambda: relay.forward(k - 3))
         between(k, 5, CHUNKS + 5, lambda: sums.forward(k - 5))
         first = jnp.where(k < 14, 2 * (k - 10), jnp.where(k == 15, 1, 4))
-        count = jnp.where((k < 10) | (k == 14), 0, jnp.where(k < 14, 1, 2))
+        count = jnp.where((k < 10) | (k > 13), 0, 1)
 
         @pl.when(k == 10)
         def _():
@@ -428,6 +428,7 @@
         between(k, 4, CHUNKS + 4, transform)
         between(k, 2, CHUNKS + 2, lambda: relay.add(k - 2))
 
+        between(k, 4, CHUNKS + 4, lambda: sums.add(k - 4))
         def settle():
             c = k - 5
             half = c // 2
@@ -442,7 +443,6 @@
                 turn(half)
                 each(1, 16, lambda n: plane_copy(half, n).start())
         between(k, 5, CHUNKS + 5, settle)
-        between(k, 4, CHUNKS + 4, lambda: sums.add(k - 4))
 
         def fill():
             make_table(k - 3)
@@ -453,7 +453,7 @@
         def _():
             gather_rows(1)
         second = jnp.where(k < 14, 2 * (k - 10) + 1, jnp.where(k == 14, 0, 3))
-        more = jnp.where((k < 10) | (k == 13) | (k == 16), 0, 1)
+        more = jnp.where((k < 10) | (k >= 13), 0, 1)
         each(second, second + more, lambda u: longitudes(jnp.where(k < 14, 0, 1), u))
         return carry
 
@@ -462,7 +462,7 @@
     pl.semaphore_wait(barrier, 18)
     lax.fori_loop(0, CHUNKS + 5, step, 0)
 
-    longitudes(1, STEPS)
+    each(0, STEPS + 1, lambda u: longitudes(1, u))
     for half in (HALVES - 2, HALVES - 1):
         each(1, 16, lambda n: plane_arrival(half, n).wait_recv())
     last_copy = pltpu.make_async_copy(lat_ref.at[pl.ds(HALVES - 2, 2)], last_ref, last_sem)

time: 218 us -> 215 us (0.986)
  Pallas kernels: 217 us -> 214 us
    pallas_call x1, Pallas kernels: 209 us -> 206 us  [flow(): pl.pallas_call(flow_kernel, name='flow', out_shape=[jax.ShapeDtypeStruct(...]
where the time goes in v9:
time: 215 us; the launch traced here: 214 us
  Pallas kernels  214 us (100%)
    pallas_call x1, Pallas kernels, flow(): pl.pallas_call(flow_kernel, name='flow', out_shape=[jax.ShapeDtypeStruct(...  206 us
    pallas_call x1, Pallas kernels, last(): pl.pallas_call(last_kernel, name='last', out_shape=jax.ShapeDtypeStruct((...  8.09 us

profile of v9, /device:TPU:1, one launch (start us, length us, event | category | flops | bytes accessed | tf_op | source)
XLA Modules:
  0.0 214.2 jit_solution(10915053339503885989)
XLA Ops:
  0.0 206.2 %flow.1 = (f32[16,2,2,4,3072]{4,3,2,1,0:T(4,128)}, bf16[2,16,4,16,128]{4,3,2,1,0:T(8,128)(2,1)}, bf16[7,16,2,16,1024]{4,3,2,1,0:T(8,128)(2,1)}) custom-call(bf16[6,1024,1024]{2,1,0:T(8,128)(2,1)} %bitcast.2, bf16[64,128,512]{2,1,0:T(8,128)(2,1)} %leg_ref.1, s32[8,128]{1,0:T(8,128)} %bitcast.3, s32[16]{0:T(128)} %selected_ref.1), custom_call_target="tpu_custom_call" | custom-call | tf_op jit(solution)/shard_map/flow/pallas_call | solution.py:494
  206.2 8.1 %last.1 = f32[16,3,2,4,3072]{4,3,2,1,0:T(4,128)} custom-call(f32[16,2,2,4,3072]{4,3,2,1,0:T(4,128)} %get-tuple-element.8.done_ref, bf16[2,16,4,16,128]{4,3,2,1,0:T(8,128)(2,1)} %get-tuple-element.9.lat_ref, bf16[7,16,2,16,1024]{4,3,2,1,0:T(8,128)(2,1)} %get-tuple-element.10.table_ref), custom_call_target="tpu_custom_call" | custom-call | tf_op jit(solution)/shard_map/last/pallas_call | solution.py:565

commit v10 on v9

--- a/solution.py
+++ b/solution.py
@@ -129,14 +129,15 @@
     for r in range(8):
         line = jnp.broadcast_to(held_ref[r:r + 1, :].astype(jnp.float32), (128, 128))
         order_ref[128 * r:128 * (r + 1), :] = line.T.astype(jnp.int32)
-    row = lax.broadcasted_iota(jnp.int32, (16, 128), 0)
-    chosen = jnp.zeros((16, 128), jnp.int32)
-    for i in range(SEL):
-        chosen = jnp.where(row == i, selected_ref[i], chosen)
-    for j in range(CS):
-        for half in range(2):
-            hit = (chosen == rad * 16 + 8 * half + lane // 16) & (lax.rem(lane, 16) == j)
-            perm_ref[16 * j:16 * (j + 1), 128 * half:128 * (half + 1)] = jnp.where(hit, 1.0, 0.0).astype(jnp.bfloat16)
+    def make_perm():
+        row = lax.broadcasted_iota(jnp.int32, (16, 128), 0)
+        chosen = jnp.zeros((16, 128), jnp.int32)
+        for i in range(SEL):
+            chosen = jnp.where(row == i, selected_ref[i], chosen)
+        for j in range(CS):
+            for half in range(2):
+                hit = (chosen == rad * 16 + 8 * half + lane // 16) & (lax.rem(lane, 16) == j)
+                perm_ref[16 * j:16 * (j + 1), 128 * half:128 * (half + 1)] = jnp.where(hit, 1.0, 0.0).astype(jnp.bfloat16)
 
     def make_pick(b):
         def body(a):
@@ -398,6 +399,10 @@
             each(1, 16, lambda n: a_copy(k, n).start())
             arecv[k, ma] = asend[lax.rem(k, 3), ma]
         between(k, 0, CHUNKS, send)
+
+        @pl.when(k == 1)
+        def _():
+            make_perm()
 
         @pl.when(k == 2)
         def _():

time: 215 us -> 215 us (level)
  no operation moved by 1% of the time
where the time goes in v10:
time: 215 us; the launch traced here: 214 us
  Pallas kernels  214 us (100%)
    pallas_call x1, Pallas kernels, flow(): pl.pallas_call(flow_kernel, name='flow', out_shape=[jax.ShapeDtypeStruct(...  206 us
    pallas_call x1, Pallas kernels, last(): pl.pallas_call(last_kernel, name='last', out_shape=jax.ShapeDtypeStruct((...  8.09 us

profile of v10, /device:TPU:1, one launch (start us, length us, event | category | flops | bytes accessed | tf_op | source)
XLA Modules:
  0.0 213.7 jit_solution(3626976386332482550)
XLA Ops:
  0.0 205.6 %flow.1 = (f32[16,2,2,4,3072]{4,3,2,1,0:T(4,128)}, bf16[2,16,4,16,128]{4,3,2,1,0:T(8,128)(2,1)}, bf16[7,16,2,16,1024]{4,3,2,1,0:T(8,128)(2,1)}) custom-call(bf16[6,1024,1024]{2,1,0:T(8,128)(2,1)} %bitcast.2, bf16[64,128,512]{2,1,0:T(8,128)(2,1)} %leg_ref.1, s32[8,128]{1,0:T(8,128)} %bitcast.3, s32[16]{0:T(128)} %selected_ref.1), custom_call_target="tpu_custom_call" | custom-call | tf_op jit(solution)/shard_map/flow/pallas_call | solution.py:499
  205.6 8.1 %last.1 = f32[16,3,2,4,3072]{4,3,2,1,0:T(4,128)} custom-call(f32[16,2,2,4,3072]{4,3,2,1,0:T(4,128)} %get-tuple-element.8.done_ref, bf16[2,16,4,16,128]{4,3,2,1,0:T(8,128)(2,1)} %get-tuple-element.9.lat_ref, bf16[7,16,2,16,1024]{4,3,2,1,0:T(8,128)(2,1)} %get-tuple-element.10.table_ref), custom_call_target="tpu_custom_call" | custom-call | tf_op jit(solution)/shard_map/last/pallas_call | solution.py:570
